TPU v7x, 32 devices: a whole 2x2x4 slice. The times are simulated.
32 devices in a mesh: seq: 2 (over x), mp: 4 (over y, core), dp: 4 (over z).
Axes of the slice: x: 2, y: 2, z: 4, core: 2. Of those that a mesh axis runs over, the one named last changes fastest.
Arguments:
- tokens: bfloat16 [16384, 2048], P(('dp', 'seq'), 'mp'), parts along dimension 0, may hold values from -6 to 6
- w_query: bfloat16 [2048, 2048], P(None, 'mp'), may hold values from -0.125 to 0.125
- w_key: bfloat16 [2048, 2048], P(None, 'mp'), may hold values from -0.125 to 0.125
- w_value: bfloat16 [2048, 2048], P(None, 'mp'), may hold values from -0.125 to 0.125
- w_gate: bfloat16 [2048, 2048], P(None, 'mp'), may hold values from -0.125 to 0.125
- decay_exponent: int32 [16], P('mp'), may hold values from 5 to 16
- forget: float32 [16384, 16], P(('dp', 'seq'), 'mp'), parts along dimension 0, may hold values from 0 to 0.69
- norm_gain: float32 [2048], replicated, may hold values from 0.1 to 1.9
Outputs:
- retained: bfloat16 [16384, 2048], P(('dp', 'seq', 'mp')), parts along dimension 0
There are 4 independent parts, one for each index of `dp`. A program takes and returns all parts, laid end to end along the dimension named above; an argument that names none is the same for every part. Nothing has to cross between parts.
All inputs are finite; a program needn't handle non-finite values.
Results may differ from a plain program's by a relative error of at most 0.015.
Values may be sent and summed in bfloat16 or wider, within the bound.
A program may use at most 64 MiB of HBM per device.

v0:
```python
import functools

import jax
import jax.numpy as jnp
from jax import lax
from jax.experimental import pallas as pl
from jax.experimental.pallas import tpu as pltpu
from jax.sharding import PartitionSpec as P

DH = 128
MESH = pl.DeviceIdType.MESH
F32 = jnp.float32
BF16 = jnp.bfloat16


def contract(a, b, dims):
    return lax.dot_general(a, b, ((dims[0], dims[1]), ((), ())), preferred_element_type=F32)


def kernel(
    n_mp, n_seq, heads, rows,
    tokens, wq, wk, wv, wg, forget, rate, gain, out,
    x, w, local_out, q_in, moved, got, sq_out, sq_got, gates, state, held, enter, state_out, state_got, offset,
    weight_sem, own_sem, y_send, y_recv, d_send, d_recv, s_send, s_recv, m_send, m_recv, q_send, q_recv,
):
    me = lax.axis_index("mp")
    place = lax.axis_index("seq")
    chips = n_mp // 2
    chip, core = me // 2, me % 2
    partner = chip * 2 + (1 - core)
    seq_rows, width = tokens.shape
    chunks = seq_rows // rows
    own_rows = seq_rows // n_mp
    parts = own_rows // rows
    head_width = width // heads

    weights = [pltpu.make_async_copy(src, w.at[i], weight_sem.at[i]) for i, src in enumerate((wq, wk, wv, wg))]

    def columns(block):
        return pl.ds(pl.multiple_of(block * width, width), width)

    def at_rows(c):
        return pl.ds(pl.multiple_of(c * rows, rows), rows)

    def own_copy(c):
        return pltpu.make_async_copy(tokens.at[at_rows(c), :], x.at[at_rows(c), columns(me)], own_sem.at[c])

    def far(step):
        return lax.rem(chip + step, chips) * 2 + core

    def back(step):
        return lax.rem(chip + chips - step, chips) * 2 + core

    def y_copy(c, step):
        return pltpu.make_async_remote_copy(
            src_ref=tokens.at[at_rows(c), :], dst_ref=x.at[at_rows(c), columns(me)],
            send_sem=y_send.at[c, step], recv_sem=y_recv.at[c, step],
            device_id={"mp": far(step)}, device_id_type=MESH)

    def y_arrival(c, step):
        return pltpu.make_async_remote_copy(
            src_ref=tokens.at[at_rows(c), :], dst_ref=x.at[at_rows(c), columns(back(step))],
            send_sem=y_send.at[c, step], recv_sem=y_recv.at[c, step],
            device_id={"mp": far(step)}, device_id_type=MESH)

    def d_copy(c, step):
        block = me if step == 0 else back(step)
        source = tokens.at[at_rows(c), :] if step == 0 else x.at[at_rows(c), columns(block)]
        return pltpu.make_async_remote_copy(
            src_ref=source, dst_ref=x.at[at_rows(c), columns(block)],
            send_sem=d_send.at[c, step], recv_sem=d_recv.at[c, step],
            device_id={"mp": partner}, device_id_type=MESH)

    def d_arrival(c, step):
        block = partner if step == 0 else lax.rem(chip + chips - step, chips) * 2 + (1 - core)
        there = x.at[at_rows(c), columns(block)]
        return pltpu.make_async_remote_copy(
            src_ref=there, dst_ref=there, send_sem=d_send.at[c, step], recv_sem=d_recv.at[c, step],
            device_id={"mp": partner}, device_id_type=MESH)

    barrier = pltpu.get_barrier_semaphore()
    for other in range(1, n_mp):
        pl.semaphore_signal(barrier, inc=1, device_id={"mp": lax.rem(me + other, n_mp)}, device_id_type=MESH)

    @pl.when(place > 0)
    def _():
        pl.semaphore_signal(barrier, inc=1, device_id={"seq": place - 1}, device_id_type=MESH)

    @pl.when(place < n_seq - 1)
    def _():
        pl.semaphore_signal(barrier, inc=1, device_id={"seq": place + 1}, device_id_type=MESH)

    for i in range(3):
        weights[i].start()
    pl.loop(0, chunks)(lambda c: own_copy(c).start())
    weights[3].start()

    neighbours = jnp.minimum(place, 1) + jnp.minimum(n_seq - 1 - place, 1)
    pl.semaphore_wait(barrier, n_mp - 1 + neighbours)

    @pl.loop(0, chunks)
    def _(c):
        for step in range(1, chips):
            y_copy(c, step).start()
        d_copy(c, 0).start()

    state[...] = jnp.zeros_like(state)
    offset[...] = jnp.zeros_like(offset)
    for i in range(3):
        weights[i].wait()

    later = lax.broadcasted_iota(jnp.int32, (rows, rows), 0)
    earlier = lax.broadcasted_iota(jnp.int32, (rows, rows), 1)
    causal = later >= earlier
    summing = (later <= earlier).astype(F32)
    exact = lax.Precision.HIGHEST

    s_copy = pltpu.make_async_remote_copy(
        src_ref=state_out, dst_ref=state_got, send_sem=s_send, recv_sem=s_recv,
        device_id={"seq": lax.rem(place + 1, n_seq)}, device_id_type=MESH)

    @pl.loop(0, chunks)
    def _(c):
        here = at_rows(c)
        for step in range(1, chips):
            y_arrival(c, step).wait_recv()
            d_copy(c, step).start()
        own_copy(c).wait()
        decay = rate[...] - forget[:, here]
        running = jnp.dot(decay, summing, precision=exact, preferred_element_type=F32)
        by_row = lax.dot_general(
            causal.astype(F32), decay, (((1,), (1,)), ((), ())), precision=exact, preferred_element_type=F32)
        last = running[:, rows - 1 :]
        before = offset[...]
        for step in range(chips):
            d_arrival(c, step).wait_recv()
        piece = x[here, :]
        key = (jnp.dot(piece, w[1], preferred_element_type=F32) * DH ** (-0.5)).astype(BF16)
        value = jnp.dot(piece, w[2], preferred_element_type=F32).astype(BF16)
        for h in range(heads):
            part = slice(h * head_width, (h + 1) * head_width)
            k, v = key[:, part], value[:, part]
            end = last[h : h + 1, :]
            grown = state[h]
            held[h] = grown.astype(BF16)
            faded = (k.astype(F32) * jnp.exp(end - by_row[:, h : h + 1])).astype(BF16)
            state[h] = jnp.exp(end) * grown + contract(faded, v, ((0,), (0,)))

        @pl.when(jnp.logical_and(place == 0, c == chunks - 1))
        def _():
            state_out[...] = state[...].astype(BF16)
            if n_seq > 1:
                s_copy.start()

        query = jnp.dot(piece, w[0], preferred_element_type=F32).astype(BF16)
        for h in range(heads):
            part = slice(h * head_width, (h + 1) * head_width)
            q, k, v = query[:, part], key[:, part], value[:, part]
            col = by_row[:, h : h + 1]
            mask = jnp.exp(jnp.where(causal, col - running[h : h + 1, :], -1e30))
            scores = (contract(q, k, ((1,), (1,))) * mask).astype(BF16)
            qf = q.astype(F32)
            carried = jnp.dot((qf * jnp.exp(col)).astype(BF16), held[h], preferred_element_type=F32)
            local_out[here, part] = jnp.dot(scores, v, preferred_element_type=F32) + carried
            q_in[here, part] = (qf * jnp.exp(col + before[h : h + 1, 0:1])).astype(BF16)
        offset[...] = before + last

    @pl.when(place == 0)
    def _():
        enter[...] = jnp.zeros_like(enter)

    def owner(o):
        t, s = o // 2, o % 2
        return lax.rem(chip + t + 1, chips) * 2 + lax.rem(core + s + (t + 1) // chips, 2)

    def gate_of(step):
        o, r = lax.rem(step, n_mp), step // n_mp
        here = at_rows(owner(o) * parts + r)
        g = jnp.dot(x[here, :], w[3], preferred_element_type=F32).astype(BF16).astype(F32)
        gates[...] = g / (1.0 + jnp.exp(-g))

    weights[3].wait()
    gate_of(0)

    @pl.when(place > 0)
    def _():
        s_copy.wait_recv()
        enter[...] = state_got[...]

    if n_seq > 2:
        @pl.when(jnp.logical_and(place > 0, place < n_seq - 1))
        def _():
            for h in range(heads):
                total = jnp.exp(offset[h : h + 1, 0:1])
                state_out[h] = (total * enter[h].astype(F32) + state[h]).astype(BF16)
            s_copy.start()

    def m_copy(o, r):
        to = owner(o)
        return pltpu.make_async_remote_copy(
            src_ref=moved.at[at_rows(to * parts + r), :], dst_ref=got.at[me, at_rows(r), :],
            send_sem=m_send.at[o, r], recv_sem=m_recv.at[me, r],
            device_id={"mp": to}, device_id_type=MESH)

    def q_copy(o, r):
        to = owner(o)
        return pltpu.make_async_remote_copy(
            src_ref=sq_out.at[to * parts + r], dst_ref=sq_got.at[me, r],
            send_sem=q_send.at[o, r], recv_sem=q_recv.at[me, r],
            device_id={"mp": to}, device_id_type=MESH)

    steps = n_mp * parts
    ones = jnp.ones((8, width), BF16)

    @pl.loop(0, steps)
    def _(step):
        o, r = lax.rem(step, n_mp), step // n_mp
        block = owner(o) * parts + r
        here = at_rows(block)
        kept = []
        for h in range(heads):
            part = slice(h * head_width, (h + 1) * head_width)
            whole = local_out[here, part] + jnp.dot(q_in[here, part], enter[h], preferred_element_type=F32)
            kept.append(whole.astype(BF16))
            moved[here, part] = (gates[:, part] * kept[h].astype(F32)).astype(BF16)

        @pl.when(o < n_mp - 1)
        def _():
            m_copy(o, r).start()

        squares = jnp.zeros((8, rows), F32)
        for h in range(heads):
            square = kept[h].astype(F32) * kept[h].astype(F32)
            high = square.astype(BF16)
            low = (square - high.astype(F32)).astype(BF16)
            unit = ones[:, h * head_width : (h + 1) * head_width]
            squares += contract(unit, high, ((1,), (1,))) + contract(unit, low, ((1,), (1,)))
        sq_out[block] = squares

        @pl.when(o < n_mp - 1)
        def _():
            q_copy(o, r).start()

        @pl.when(o == n_mp - 1)
        def _():
            got[me, at_rows(r), :] = moved[here, :]
            sq_got[me, r] = squares

        @pl.when(step < steps - 1)
        def _():
            gate_of(step + 1)

    def m_arrival(source, r):
        there = got.at[source, at_rows(r), :]
        return pltpu.make_async_remote_copy(
            src_ref=there, dst_ref=there, send_sem=m_send.at[0, r], recv_sem=m_recv.at[source, r],
            device_id={"mp": partner}, device_id_type=MESH)

    def q_arrival(source, r):
        there = sq_got.at[source, r]
        return pltpu.make_async_remote_copy(
            src_ref=there, dst_ref=there, send_sem=q_send.at[0, r], recv_sem=q_recv.at[source, r],
            device_id={"mp": partner}, device_id_type=MESH)

    for r in range(parts):
        for other in range(1, n_mp):
            source = lax.rem(me + other, n_mp)
            q_arrival(source, r).wait_recv()
            m_arrival(source, r).wait_recv()
        total = sq_got[0, r]
        for source in range(1, n_mp):
            total += sq_got[source, r]
        scale = lax.rsqrt(total * (1.0 / (n_mp * width)) + 1e-06).T[:, 0:1]
        span = slice(r * rows, (r + 1) * rows)
        for source in range(n_mp):
            part = slice(source * width, (source + 1) * width)
            out[span, part] = (got[source, span, :].astype(F32) * scale * gain[:, part]).astype(BF16)

    @pl.loop(0, chunks)
    def _(c):
        for step in range(1, chips):
            y_copy(c, step).wait_send()
        for step in range(chips):
            d_copy(c, step).wait_send()

    @pl.loop(0, n_mp - 1)
    def _(o):
        for r in range(parts):
            q_copy(o, r).wait_send()
            m_copy(o, r).wait_send()

    if n_seq > 1:
        @pl.when(place < n_seq - 1)
        def _():
            s_copy.wait_send()


def body(n_mp, n_seq, tokens, w_query, w_key, w_value, w_gate, decay_exponent, forget, norm_gain):
    seq_rows, width = tokens.shape
    features = w_query.shape[0]
    heads = decay_exponent.shape[0]
    own_rows = seq_rows // n_mp
    rows = 256 if own_rows % 256 == 0 else own_rows
    chunks, parts = seq_rows // rows, own_rows // rows
    rate = jnp.log1p(-jnp.exp2(-decay_exponent.astype(F32)))
    hbm, vmem = pl.BlockSpec(memory_space=pl.ANY), pl.BlockSpec(memory_space=pltpu.VMEM)
    dma = pltpu.SemaphoreType.DMA
    chips = n_mp // 2
    return pl.pallas_call(
        functools.partial(kernel, n_mp, n_seq, heads, rows),
        out_shape=jax.ShapeDtypeStruct((own_rows, features), BF16),
        in_specs=[hbm] * 5 + [vmem] * 3,
        out_specs=vmem,
        scratch_shapes=[
            pltpu.VMEM((seq_rows, features), BF16),
            pltpu.VMEM((4, features, width), BF16),
            pltpu.VMEM((seq_rows, width), F32),
            pltpu.VMEM((seq_rows, width), BF16),
            pltpu.VMEM((seq_rows, width), BF16),
            pltpu.VMEM((n_mp, own_rows, width), BF16),
            pltpu.VMEM((chunks, 8, rows), F32),
            pltpu.VMEM((n_mp, parts, 8, rows), F32),
            pltpu.VMEM((rows, width), F32),
            pltpu.VMEM((heads, DH, DH), F32),
            pltpu.VMEM((heads, DH, DH), BF16),
            pltpu.VMEM((heads, DH, DH), BF16),
            pltpu.VMEM((heads, DH, DH), BF16),
            pltpu.VMEM((heads, DH, DH), BF16),
            pltpu.VMEM((heads, 128), F32),
            dma((4,)),
            dma((chunks,)),
            dma((chunks, chips)),
            dma((chunks, chips)),
            dma((chunks, chips)),
            dma((chunks, chips)),
            dma,
            dma,
            dma((n_mp, parts)),
            dma((n_mp, parts)),
            dma((n_mp, parts)),
            dma((n_mp, parts)),
        ],
        compiler_params=pltpu.CompilerParams(
            collective_id=0, has_side_effects=True, vmem_limit_bytes=60 * 1024 * 1024
        ),
    )(tokens, w_query, w_key, w_value, w_gate, forget.T, rate[:, None], norm_gain[None, :])


def solution(mesh):
    placed = (
        P(("dp", "seq"), "mp"),
        P(None, "mp"),
        P(None, "mp"),
        P(None, "mp"),
        P(None, "mp"),
        P("mp"),
        P(("dp", "seq"), "mp"),
        P(),
    )
    return jax.shard_map(
        functools.partial(body, mesh.shape["mp"], mesh.shape["seq"]),
        mesh=mesh,
        in_specs=placed,
        out_specs=P(("dp", "seq", "mp"), None),
        check_vma=False,
    )
```

profile of v0, /device:TPU:19, one launch (start us, length us, event | category | flops | bytes accessed | tf_op | source)
XLA Modules:
  0.0 89.0 jit_solution(18027673448184256589)
XLA Ops:
  0.0 0.7 log-plus-one_bitcast_fusion
  0.7 0.7 copy.9.rate
  1.3 84.5 %shard_map.82 = bf16[512,2048]{1,0:T(8,128)(2,1)} custom-call(bf16[2048,512]{1,0:T(8,128)(2,1)} %tokens.1, bf16[2048,512]{1,0:T(8,128)(2,1)} %wq.1, bf16[2048,512]{1,0:T(8,128)(2,1)} %wk.1, bf16[2048,512]{1,0:T(8,128)(2,1)} %wv.1, bf16[2048,512]{1,0:T(8,128)(2,1)} %wg.1, f32[4,2048]{1,0:T(4,128)} %bitcast.4, f32[4,1]{1,0:T(4,128)} %copy.9.rate, ...), custom_call_target="tpu_custom_call" | custom-call | tf_op jit(solution)/shard_map/pallas_call | solution.py:309
  85.8 3.2 %copy.11 = bf16[512,2048]{1,0:T(8,128)(2,1)} copy(bf16[512,2048]{1,0:T(8,128)(2,1)} %shard_map.82) | data formatting | bytes 4194304
where the time goes:
time: 89.2 us; the launch traced here: 89 us
  Pallas kernels  84.5 us (95%)
  local copies, waits for them, and re-layouts  3.83 us (4%)
    pallas_call x1, Pallas kernels, body(): pl.pallas_call(functools.partial(kernel, n_mp, n_seq, heads, rows), out_s...  84.5 us
    unnamed x1, local copies, waits for them, and re-layouts  3.16 us

commit v1 on v0

v1 whole, which is shorter than its diff:
```python
import functools

import jax
import jax.numpy as jnp
from jax import lax
from jax.experimental import pallas as pl
from jax.experimental.pallas import tpu as pltpu
from jax.sharding import PartitionSpec as P

DH = 128
MESH = pl.DeviceIdType.MESH
F32 = jnp.float32
BF16 = jnp.bfloat16


def contract(a, b, dims):
    return lax.dot_general(a, b, ((dims[0], dims[1]), ((), ())), preferred_element_type=F32)


def kernel(
    n_mp, n_seq, heads, rows, groups,
    tokens, wq, wk, wv, wg, exponent_in, forget_in, gain_in, out,
    x, w, exponent, forget, gain, partial, local_out, q_in, gates, moved, got, sq_out, sq_got,
    state, held, enter, state_out, state_got, offset,
    weight_sem, small_sem, own_sem, y_send, y_recv, d_send, d_recv, s_send, s_recv, m_send, m_recv, q_send, q_recv,
):
    me = lax.axis_index("mp")
    place = lax.axis_index("seq")
    chips = n_mp // 2
    chip, core = me // 2, me % 2
    partner = chip * 2 + (1 - core)
    seq_rows, width = tokens.shape
    chunks = seq_rows // rows
    own_rows = seq_rows // n_mp
    parts = own_rows // rows
    head_width = width // heads
    group_heads = heads // groups
    group_width = width // groups

    barrier = pltpu.get_barrier_semaphore()
    for other in range(1, n_mp):
        pl.semaphore_signal(barrier, inc=1, device_id={"mp": lax.rem(me + other, n_mp)}, device_id_type=MESH)

    @pl.when(place > 0)
    def _():
        pl.semaphore_signal(barrier, inc=1, device_id={"seq": place - 1}, device_id_type=MESH)

    @pl.when(place < n_seq - 1)
    def _():
        pl.semaphore_signal(barrier, inc=1, device_id={"seq": place + 1}, device_id_type=MESH)

    weights = [pltpu.make_async_copy(src, w.at[i], weight_sem.at[i]) for i, src in enumerate((wk, wv, wq, wg))]
    small = [
        pltpu.make_async_copy(src, dst, small_sem.at[i])
        for i, (src, dst) in enumerate(((exponent_in, exponent), (forget_in, forget), (gain_in, gain)))
    ]

    def columns(block):
        return pl.ds(pl.multiple_of(block * width, width), width)

    def at_rows(c):
        return pl.ds(pl.multiple_of(c * rows, rows), rows)

    def own_copy(c):
        return pltpu.make_async_copy(tokens.at[at_rows(c), :], x.at[at_rows(c), columns(me)], own_sem.at[c])

    def far(step):
        return lax.rem(chip + step, chips) * 2 + core

    def back(step):
        return lax.rem(chip + chips - step, chips) * 2 + core

    def back_other(step):
        return lax.rem(chip + chips - step, chips) * 2 + (1 - core)

    def y_copy(c, step):
        return pltpu.make_async_remote_copy(
            src_ref=tokens.at[at_rows(c), :], dst_ref=x.at[at_rows(c), columns(me)],
            send_sem=y_send.at[c, step], recv_sem=y_recv.at[c, step],
            device_id={"mp": far(step)}, device_id_type=MESH)

    def y_arrival(c, step):
        return pltpu.make_async_remote_copy(
            src_ref=tokens.at[at_rows(c), :], dst_ref=x.at[at_rows(c), columns(back(step))],
            send_sem=y_send.at[c, step], recv_sem=y_recv.at[c, step],
            device_id={"mp": far(step)}, device_id_type=MESH)

    def d_copy(c, step):
        block = me if step == 0 else back(step)
        source = tokens.at[at_rows(c), :] if step == 0 else x.at[at_rows(c), columns(block)]
        return pltpu.make_async_remote_copy(
            src_ref=source, dst_ref=x.at[at_rows(c), columns(block)],
            send_sem=d_send.at[c, step], recv_sem=d_recv.at[c, step],
            device_id={"mp": partner}, device_id_type=MESH)

    def d_arrival(c, step):
        there = x.at[at_rows(c), columns(partner if step == 0 else back_other(step))]
        return pltpu.make_async_remote_copy(
            src_ref=there, dst_ref=there, send_sem=d_send.at[c, step], recv_sem=d_recv.at[c, step],
            device_id={"mp": partner}, device_id_type=MESH)

    for copy in small:
        copy.start()
    own_copy(0).start()
    for copy in weights:
        copy.start()
    pl.loop(1, chunks)(lambda c: own_copy(c).start())

    neighbours = jnp.minimum(place, 1) + jnp.minimum(n_seq - 1 - place, 1)
    pl.semaphore_wait(barrier, n_mp - 1 + neighbours)

    @pl.loop(0, chunks)
    def _(c):
        for step in range(1, chips):
            y_copy(c, step).start()
        d_copy(c, 0).start()

    state[...] = jnp.zeros_like(state)
    offset[...] = jnp.zeros_like(offset)
    enter[...] = jnp.zeros_like(enter)

    later = lax.broadcasted_iota(jnp.int32, (rows, rows), 0)
    earlier = lax.broadcasted_iota(jnp.int32, (rows, rows), 1)
    causal = later >= earlier
    summing = (later <= earlier).astype(F32)
    exact = lax.Precision.HIGHEST
    ones = jnp.ones((8, head_width), BF16)

    for copy in small:
        copy.wait()
    spread = jnp.broadcast_to(exponent[...].astype(F32), (heads, heads))
    diagonal = lax.broadcasted_iota(jnp.int32, (heads, heads), 0) == lax.broadcasted_iota(jnp.int32, (heads, heads), 1)
    column = jnp.sum(jnp.where(diagonal, spread, 0.0), axis=1, keepdims=True)
    rate = jnp.log1p(-jnp.exp2(-column))
    for copy in weights:
        copy.wait()

    def s_copy(g):
        part = pl.ds(g * group_heads, group_heads)
        return pltpu.make_async_remote_copy(
            src_ref=state_out.at[part], dst_ref=state_got.at[part], send_sem=s_send.at[g], recv_sem=s_recv.at[g],
            device_id={"seq": lax.rem(place + 1, n_seq)}, device_id_type=MESH)

    def group_columns(g):
        return pl.ds(g * group_width, group_width)

    def m_copy(block, g):
        to, r = block // parts, lax.rem(block, parts)
        return pltpu.make_async_remote_copy(
            src_ref=moved.at[at_rows(block), group_columns(g)], dst_ref=got.at[me, at_rows(r), group_columns(g)],
            send_sem=m_send.at[block, g], recv_sem=m_recv.at[me, r, g],
            device_id={"mp": to}, device_id_type=MESH)

    def q_copy(block):
        to, r = block // parts, lax.rem(block, parts)
        return pltpu.make_async_remote_copy(
            src_ref=sq_out.at[block], dst_ref=sq_got.at[me, r],
            send_sem=q_send.at[block], recv_sem=q_recv.at[me, r],
            device_id={"mp": to}, device_id_type=MESH)

    def finalize(block, g):
        here = at_rows(block)
        to, r = block // parts, lax.rem(block, parts)
        squares = jnp.zeros((8, rows), F32)
        for h in range(g * group_heads, (g + 1) * group_heads):
            part = slice(h * head_width, (h + 1) * head_width)
            whole = local_out[here, part] + jnp.dot(q_in[here, part], enter[h], preferred_element_type=F32)
            kept = whole.astype(BF16).astype(F32)
            moved[here, part] = (gates[here, part] * kept).astype(BF16)
            square = kept * kept
            high = square.astype(BF16)
            low = (square - high.astype(F32)).astype(BF16)
            squares += contract(ones, high, ((1,), (1,))) + contract(ones, low, ((1,), (1,)))
        total = squares[0:1, :]
        if g > 0:
            total = total + sq_out[block]
        sq_out[block] = total

        @pl.when(to != me)
        def _():
            if g == groups - 1:
                q_copy(block).start()
            m_copy(block, g).start()

        @pl.when(to == me)
        def _():
            part = slice(g * group_width, (g + 1) * group_width)
            got[me, at_rows(r), part] = moved[here, part]
            if g == groups - 1:
                sq_got[me, r] = total

    @pl.loop(0, chunks)
    def _(c):
        here = at_rows(c)
        decay = rate - forget[:, here]
        running = jnp.dot(decay, summing, precision=exact, preferred_element_type=F32)
        by_row = lax.dot_general(
            causal.astype(F32), decay, (((1,), (1,)), ((), ())), precision=exact, preferred_element_type=F32)
        last = running[:, rows - 1 :]
        before = offset[...]

        own_copy(c).wait()
        d_arrival(c, 0).wait_recv()
        own_side = pl.ds(pl.multiple_of(chip * 2 * width, 2 * width), 2 * width)
        piece = x[here, own_side]
        for i in range(4):
            partial[i] = jnp.dot(piece, w[i, own_side, :], preferred_element_type=F32)
        for step in range(1, chips):
            y_arrival(c, step).wait_recv()
            d_copy(c, step).start()
        for step in range(1, chips):
            piece = x[here, columns(back(step))]
            for i in range(4):
                partial[i] += jnp.dot(piece, w[i, columns(back(step)), :], preferred_element_type=F32)
        for step in range(1, chips):
            d_arrival(c, step).wait_recv()

        def project(i):
            total = partial[i]
            for step in range(1, chips):
                total += jnp.dot(
                    x[here, columns(back_other(step))], w[i, columns(back_other(step)), :],
                    preferred_element_type=F32)
            return total

        key = (project(0) * DH ** (-0.5)).astype(BF16)
        value = project(1).astype(BF16)
        for h in range(heads):
            part = slice(h * head_width, (h + 1) * head_width)
            k, v = key[:, part], value[:, part]
            end = last[h : h + 1, :]
            grown = state[h]
            held[h] = grown.astype(BF16)
            faded = (k.astype(F32) * jnp.exp(end - by_row[:, h : h + 1])).astype(BF16)
            state[h] = jnp.exp(end) * grown + contract(faded, v, ((0,), (0,)))

        @pl.when(jnp.logical_and(place == 0, c == chunks - 1))
        def _():
            state_out[...] = state[...].astype(BF16)
            if n_seq > 1:
                for g in range(groups):
                    s_copy(g).start()

        query = project(2).astype(BF16)
        for h in range(heads):
            part = slice(h * head_width, (h + 1) * head_width)
            q, k, v = query[:, part], key[:, part], value[:, part]
            col = by_row[:, h : h + 1]
            mask = jnp.exp(jnp.where(causal, col - running[h : h + 1, :], -1e30))
            scores = (contract(q, k, ((1,), (1,))) * mask).astype(BF16)
            qf = q.astype(F32)
            carried = jnp.dot((qf * jnp.exp(col)).astype(BF16), held[h], preferred_element_type=F32)
            local_out[here, part] = jnp.dot(scores, v, preferred_element_type=F32) + carried
            q_in[here, part] = (qf * jnp.exp(col + before[h : h + 1, 0:1])).astype(BF16)
        offset[...] = before + last
        gate = project(3).astype(BF16).astype(F32)
        gates[here, :] = gate / (1.0 + jnp.exp(-gate))

        @pl.when(place == 0)
        def _():
            for g in range(groups):
                finalize(c, g)

    far_steps = (n_mp - 2) * parts

    def in_order(step):
        o = lax.rem(step, n_mp - 2)
        away = (lax.rem(chip + o // 2 + 1, chips) * 2 + lax.rem(core + o, 2)) * parts + step // (n_mp - 2)
        rest = jnp.maximum(step - far_steps, 0)
        home = (chip * 2 + lax.rem(core + 1 + rest, 2)) * parts + rest // 2
        return jnp.where(step < far_steps, away, home)

    if n_seq > 1:
        @pl.when(place > 0)
        def _():
            for g in range(groups):
                part = slice(g * group_heads, (g + 1) * group_heads)
                s_copy(g).wait_recv()
                enter[part] = state_got[part]
                if n_seq > 2:
                    @pl.when(place < n_seq - 1)
                    def _():
                        for h in range(g * group_heads, (g + 1) * group_heads):
                            total = jnp.exp(offset[h : h + 1, 0:1])
                            state_out[h] = (total * enter[h].astype(F32) + state[h]).astype(BF16)
                        s_copy(g).start()

                pl.loop(0, chunks)(lambda step: finalize(in_order(step), g))

    def m_arrival(source, r, g):
        there = got.at[source, at_rows(r), group_columns(g)]
        return pltpu.make_async_remote_copy(
            src_ref=there, dst_ref=there, send_sem=m_send.at[0, 0], recv_sem=m_recv.at[source, r, g],
            device_id={"mp": partner}, device_id_type=MESH)

    def q_arrival(source, r):
        there = sq_got.at[source, r]
        return pltpu.make_async_remote_copy(
            src_ref=there, dst_ref=there, send_sem=q_send.at[0], recv_sem=q_recv.at[source, r],
            device_id={"mp": partner}, device_id_type=MESH)

    sources = [me, partner] + [lax.rem(chip + t, chips) * 2 + lax.rem(core + s, 2) for t in range(1, chips) for s in (0, 1)]

    for r in range(parts):
        for source in sources[1:]:
            q_arrival(source, r).wait_recv()
        total = sq_got[0, r]
        for source in range(1, n_mp):
            total += sq_got[source, r]
        scale = lax.rsqrt(total * (1.0 / (n_mp * width)) + 1e-06)
        scale = jnp.broadcast_to(scale, (8, rows)).T[:, 0:1]
        span = slice(r * rows, (r + 1) * rows)
        for g in range(groups):
            for i, source in enumerate(sources):
                if i > 0:
                    m_arrival(source, r, g).wait_recv()
                part = pl.ds(pl.multiple_of(source * width + g * group_width, group_width), group_width)
                piece = got[source, span, g * group_width : (g + 1) * group_width].astype(F32)
                out[span, part] = (piece * scale * gain[:, part]).astype(BF16)

    @pl.loop(0, chunks)
    def _(c):
        for step in range(1, chips):
            y_copy(c, step).wait_send()
        for step in range(chips):
            d_copy(c, step).wait_send()

        @pl.when(c // parts != me)
        def _():
            q_copy(c).wait_send()
            for g in range(groups):
                m_copy(c, g).wait_send()

    if n_seq > 1:
        @pl.when(place < n_seq - 1)
        def _():
            for g in range(groups):
                s_copy(g).wait_send()


def body(n_mp, n_seq, tokens, w_query, w_key, w_value, w_gate, decay_exponent, forget, norm_gain):
    seq_rows, width = tokens.shape
    features = w_query.shape[0]
    heads = decay_exponent.shape[0]
    own_rows = seq_rows // n_mp
    rows = 256 if own_rows % 256 == 0 else own_rows
    chunks, parts = seq_rows // rows, own_rows // rows
    groups = 2 if heads % 2 == 0 else 1
    hbm = pl.BlockSpec(memory_space=pl.ANY)
    dma = pltpu.SemaphoreType.DMA
    chips = n_mp // 2
    return pl.pallas_call(
        functools.partial(kernel, n_mp, n_seq, heads, rows, groups),
        out_shape=pltpu.VMEM((own_rows, features), BF16),
        in_specs=[hbm] * 8,
        out_specs=pl.BlockSpec(memory_space=pltpu.VMEM),
        scratch_shapes=[
            pltpu.VMEM((seq_rows, features), BF16),
            pltpu.VMEM((4, features, width), BF16),
            pltpu.VMEM((1, heads), jnp.int32),
            pltpu.VMEM((heads, seq_rows), F32),
            pltpu.VMEM((1, features), F32),
            pltpu.VMEM((4, rows, width), F32),
            pltpu.VMEM((seq_rows, width), F32),
            pltpu.VMEM((seq_rows, width), BF16),
            pltpu.VMEM((seq_rows, width), F32),
            pltpu.VMEM((seq_rows, width), BF16),
            pltpu.VMEM((n_mp, own_rows, width), BF16),
            pltpu.VMEM((chunks, 1, rows), F32),
            pltpu.VMEM((n_mp, parts, 1, rows), F32),
            pltpu.VMEM((heads, DH, DH), F32),
            pltpu.VMEM((heads, DH, DH), BF16),
            pltpu.VMEM((heads, DH, DH), BF16),
            pltpu.VMEM((heads, DH, DH), BF16),
            pltpu.VMEM((heads, DH, DH), BF16),
            pltpu.VMEM((heads, 128), F32),
            dma((4,)),
            dma((3,)),
            dma((chunks,)),
            dma((chunks, chips)),
            dma((chunks, chips)),
            dma((chunks, chips)),
            dma((chunks, chips)),
            dma((groups,)),
            dma((groups,)),
            dma((chunks, groups)),
            dma((n_mp, parts, groups)),
            dma((chunks,)),
            dma((n_mp, parts)),
        ],
        compiler_params=pltpu.CompilerParams(
            collective_id=0, has_side_effects=True, vmem_limit_bytes=48 * 1024 * 1024
        ),
    )(tokens, w_query, w_key, w_value, w_gate, decay_exponent[None, :], forget.T, norm_gain[None, :])


def solution(mesh):
    placed = (
        P(("dp", "seq"), "mp"),
        P(None, "mp"),
        P(None, "mp"),
        P(None, "mp"),
        P(None, "mp"),
        P("mp"),
        P(("dp", "seq"), "mp"),
        P(),
    )
    return jax.shard_map(
        functools.partial(body, mesh.shape["mp"], mesh.shape["seq"]),
        mesh=mesh,
        in_specs=placed,
        out_specs=P(("dp", "seq", "mp"), None),
        check_vma=False,
    )
```

time: 89.2 us -> 85.4 us (0.957)
  Pallas kernels: 84.5 us -> 80.1 us
  local copies, waits for them, and re-layouts: 3.83 us -> 5.02 us
    pallas_call x1, Pallas kernels: 84.5 us -> 80.1 us  [body(): pl.pallas_call(functools.partial(kernel, n_mp, n_seq, heads, rows, groups...]
    unnamed x1 -> x9, local copies, waits for them, and re-layouts: 3.16 us -> 5.02 us
where the time goes in v1:
time: 85.4 us; the launch traced here: 85.2 us
  Pallas kernels  80.1 us (94%)
  local copies, waits for them, and re-layouts  5.02 us (6%)
    pallas_call x1, Pallas kernels, body(): pl.pallas_call(functools.partial(kernel, n_mp, n_seq, heads, rows, groups...  80.1 us
    unnamed x9, local copies, waits for them, and re-layouts  5.02 us

profile of v1, /device:TPU:19, one launch (start us, length us, event | category | flops | bytes accessed | tf_op | source)
XLA Modules:
  0.0 85.2 jit_solution(10794521497333409203)
XLA Ops:
  0.0 0.0 copy-start
  0.0 1.6 %copy-done = bf16[2048,512]{1,0:T(8,128)(2,1)S(1)} copy-done((bf16[2048,512]{1,0:T(8,128)(2,1)S(1)}, bf16[2048,512]{1,0:T(8,128)(2,1)}, u32[]{:S(2)}) %copy-start) | copy-done | bytes 2097176
  1.6 0.0 copy-start.1
  1.6 0.8 copy-done.1
  2.4 0.0 copy-start.2
  2.4 0.7 copy-done.2
  3.0 0.0 copy-start.3
  3.0 0.7 copy-done.3
  3.7 80.1 %shard_map.82 = bf16[512,2048]{1,0:T(8,128)(2,1)S(1)} custom-call(bf16[2048,512]{1,0:T(8,128)(2,1)S(1)} %copy-done, bf16[2048,512]{1,0:T(8,128)(2,1)} %wq.1, bf16[2048,512]{1,0:T(8,128)(2,1)} %wk.1, bf16[2048,512]{1,0:T(8,128)(2,1)} %wv.1, bf16[2048,512]{1,0:T(8,128)(2,1)} %wg.1, s32[1,4]{1,0:T(1,128)S(1)} %bitcast.5, f32[4,2048]{1,0:T(4,128)S(1)} %bitcast.3, ...), custom_call_target="tpu_custom_call" | custom-call | tf_op jit(solution)/shard_map/pallas_call | solution.py:352
  83.8 1.3 %copy.10 = bf16[512,2048]{1,0:T(8,128)(2,1)} copy(bf16[512,2048]{1,0:T(8,128)(2,1)S(1)} %shard_map.82) | data formatting | bytes 4194304
Async XLA Ops:
  0.0 1.6 %copy-start = (bf16[2048,512]{1,0:T(8,128)(2,1)S(1)}, bf16[2048,512]{1,0:T(8,128)(2,1)}, u32[]{:S(2)}) copy-start(bf16[2048,512]{1,0:T(8,128)(2,1)} %tokens.1) | copy-start | bytes 6291460
  1.6 0.8 copy-start.1
  2.4 0.7 copy-start.2
  3.0 0.7 copy-start.3

commit v2 on v1

--- a/solution.py
+++ b/solution.py
@@ -21,8 +21,8 @@
     n_mp, n_seq, heads, rows, groups,
     tokens, wq, wk, wv, wg, exponent_in, forget_in, gain_in, out,
     x, w, exponent, forget, gain, partial, local_out, q_in, gates, moved, got, sq_out, sq_got,
-    state, held, enter, state_out, state_got, offset,
-    weight_sem, small_sem, own_sem, y_send, y_recv, d_send, d_recv, s_send, s_recv, m_send, m_recv, q_send, q_recv,
+    state, held, enter, state_out, state_got, offset, hop_in, hop_out,
+    weight_sem, small_sem, own_sem, y_send, y_recv, d_send, d_recv, s_send, s_recv, m_send, m_recv, q_send, q_recv, hop_send, hop_recv,
 ):
     me = lax.axis_index("mp")
     place = lax.axis_index("seq")
@@ -36,6 +36,11 @@
     head_width = width // heads
     group_heads = heads // groups
     group_width = width // groups
+    relay = n_seq == 2 and chips == 2
+    hop_rows = hop_in.shape[0]
+    tail_rows = pl.ds(seq_rows - hop_rows, hop_rows)
+    head_rows = pl.ds(seq_rows - rows, rows - hop_rows)
+    across = lax.rem(chip + 1, chips) * 2 + core
 
     barrier = pltpu.get_barrier_semaphore()
     for other in range(1, n_mp):
@@ -48,6 +53,9 @@
     @pl.when(place < n_seq - 1)
     def _():
         pl.semaphore_signal(barrier, inc=1, device_id={"seq": place + 1}, device_id_type=MESH)
+
+    if relay:
+        pl.semaphore_signal(barrier, inc=1, device_id={"mp": across, "seq": 1 - place}, device_id_type=MESH)
 
     weights = [pltpu.make_async_copy(src, w.at[i], weight_sem.at[i]) for i, src in enumerate((wk, wv, wq, wg))]
     small = [
@@ -98,6 +106,30 @@
         return pltpu.make_async_remote_copy(
             src_ref=there, dst_ref=there, send_sem=d_send.at[c, step], recv_sem=d_recv.at[c, step],
             device_id={"mp": partner}, device_id_type=MESH)
+
+    def hop_copy(i):
+        if i == 0:
+            source, there, to = tokens.at[tail_rows, :], hop_in, {"mp": across, "seq": 1}
+        elif i == 1:
+            source, there, to = hop_in, x.at[tail_rows, columns(across)], {"seq": 0}
+        else:
+            source, there, to = hop_out, got.at[across, at_rows(0), pl.ds(0, group_width)], {"seq": 1}
+        arrival = (hop_recv.at[0], y_recv.at[chunks - 1, 1], m_recv.at[across, 0, 0])[i]
+        return pltpu.make_async_remote_copy(
+            src_ref=source, dst_ref=there, send_sem=hop_send.at[i], recv_sem=arrival,
+            device_id=to, device_id_type=MESH)
+
+    def y_short():
+        return pltpu.make_async_remote_copy(
+            src_ref=tokens.at[head_rows, :], dst_ref=x.at[head_rows, columns(me)],
+            send_sem=y_send.at[chunks - 1, 1], recv_sem=y_recv.at[chunks - 1, 1],
+            device_id={"mp": across}, device_id_type=MESH)
+
+    def out_hop(block):
+        return pltpu.make_async_remote_copy(
+            src_ref=moved.at[at_rows(block), pl.ds(0, group_width)], dst_ref=hop_out,
+            send_sem=m_send.at[block, 0], recv_sem=hop_recv.at[1],
+            device_id={"mp": across, "seq": 0}, device_id_type=MESH)
 
     for copy in small:
         copy.start()
@@ -107,13 +139,29 @@
     pl.loop(1, chunks)(lambda c: own_copy(c).start())
 
     neighbours = jnp.minimum(place, 1) + jnp.minimum(n_seq - 1 - place, 1)
-    pl.semaphore_wait(barrier, n_mp - 1 + neighbours)
-
-    @pl.loop(0, chunks)
+    pl.semaphore_wait(barrier, n_mp - 1 + neighbours + (1 if relay else 0))
+
+    if relay:
+        @pl.when(place == 0)
+        def _():
+            hop_copy(0).start()
+
+    @pl.loop(0, chunks - 1 if relay else chunks)
     def _(c):
         for step in range(1, chips):
             y_copy(c, step).start()
         d_copy(c, 0).start()
+
+    if relay:
+        @pl.when(place == 0)
+        def _():
+            y_short().start()
+
+        @pl.when(place == 1)
+        def _():
+            y_copy(chunks - 1, 1).start()
+
+        d_copy(chunks - 1, 0).start()
 
     state[...] = jnp.zeros_like(state)
     offset[...] = jnp.zeros_like(offset)
@@ -158,7 +206,7 @@
             send_sem=q_send.at[block], recv_sem=q_recv.at[me, r],
             device_id={"mp": to}, device_id_type=MESH)
 
-    def finalize(block, g):
+    def finalize(block, g, detour=False):
         here = at_rows(block)
         to, r = block // parts, lax.rem(block, parts)
         squares = jnp.zeros((8, rows), F32)
@@ -180,7 +228,7 @@
         def _():
             if g == groups - 1:
                 q_copy(block).start()
-            m_copy(block, g).start()
+            (out_hop(block) if detour else m_copy(block, g)).start()
 
         @pl.when(to == me)
         def _():
@@ -205,6 +253,12 @@
         piece = x[here, own_side]
         for i in range(4):
             partial[i] = jnp.dot(piece, w[i, own_side, :], preferred_element_type=F32)
+        if relay:
+            @pl.when(jnp.logical_and(place == 1, c == chunks // 4))
+            def _():
+                hop_copy(0).wait_recv()
+                hop_copy(1).start()
+
         for step in range(1, chips):
             y_arrival(c, step).wait_recv()
             d_copy(c, step).start()
@@ -285,7 +339,16 @@
                             state_out[h] = (total * enter[h].astype(F32) + state[h]).astype(BF16)
                         s_copy(g).start()
 
-                pl.loop(0, chunks)(lambda step: finalize(in_order(step), g))
+                detour = relay and g == 0
+                if detour:
+                    finalize(in_order(0), g, True)
+                pl.loop(1 if detour else 0, chunks)(lambda step: finalize(in_order(step), g))
+
+    if relay:
+        @pl.when(place == 0)
+        def _():
+            out_hop(0).wait_recv()
+            hop_copy(2).start()
 
     def m_arrival(source, r, g):
         there = got.at[source, at_rows(r), group_columns(g)]
@@ -321,7 +384,10 @@
     @pl.loop(0, chunks)
     def _(c):
         for step in range(1, chips):
-            y_copy(c, step).wait_send()
+            if relay:
+                pl.when(c < chunks - 1)(lambda: y_copy(c, step).wait_send())
+            else:
+                y_copy(c, step).wait_send()
         for step in range(chips):
             d_copy(c, step).wait_send()
 
@@ -336,6 +402,22 @@
         def _():
             for g in range(groups):
                 s_copy(g).wait_send()
+
+    if relay:
+        @pl.when(place == 0)
+        def _():
+            y_short().wait_send()
+            hop_copy(0).wait_send()
+            hop_copy(2).wait_send()
+
+        @pl.when(place == 1)
+        def _():
+            y_copy(chunks - 1, 1).wait_send()
+            hop_copy(1).wait_send()
+
+
+def in_hbm(a):
+    return a if a.size == 1 else pltpu.with_memory_space_constraint(a, pltpu.HBM)
 
 
 def body(n_mp, n_seq, tokens, w_query, w_key, w_value, w_gate, decay_exponent, forget, norm_gain):
@@ -346,7 +428,7 @@
     rows = 256 if own_rows % 256 == 0 else own_rows
     chunks, parts = seq_rows // rows, own_rows // rows
     groups = 2 if heads % 2 == 0 else 1
-    hbm = pl.BlockSpec(memory_space=pl.ANY)
+    hbm = pl.BlockSpec(memory_space=pltpu.HBM)
     dma = pltpu.SemaphoreType.DMA
     chips = n_mp // 2
     return pl.pallas_call(
@@ -374,6 +456,8 @@
             pltpu.VMEM((heads, DH, DH), BF16),
             pltpu.VMEM((heads, DH, DH), BF16),
             pltpu.VMEM((heads, 128), F32),
+            pltpu.VMEM((rows // 2, width), BF16),
+            pltpu.VMEM((rows, width // groups), BF16),
             dma((4,)),
             dma((3,)),
             dma((chunks,)),
@@ -387,11 +471,13 @@
             dma((n_mp, parts, groups)),
             dma((chunks,)),
             dma((n_mp, parts)),
+            dma((3,)),
+            dma((2,)),
         ],
         compiler_params=pltpu.CompilerParams(
             collective_id=0, has_side_effects=True, vmem_limit_bytes=48 * 1024 * 1024
         ),
-    )(tokens, w_query, w_key, w_value, w_gate, decay_exponent[None, :], forget.T, norm_gain[None, :])
+    )(*(in_hbm(a) for a in (tokens, w_query, w_key, w_value, w_gate, decay_exponent[None, :], forget.T, norm_gain[None, :])))
 
 
 def solution(mesh):

time: 85.4 us -> 80.3 us (0.940)
  local copies, waits for them, and re-layouts: 5.02 us -> 1.32 us
  Pallas kernels: 80.1 us -> 78.8 us
    unnamed x9 -> x1, local copies, waits for them, and re-layouts: 5.02 us -> 1.32 us
    pallas_call x1, Pallas kernels: 80.1 us -> 78.8 us  [body(): pl.pallas_call(functools.partial(kernel, n_mp, n_seq, heads, rows, groups...]
where the time goes in v2:
time: 80.3 us; the launch traced here: 80.2 us
  Pallas kernels  78.8 us (98%)
  local copies, waits for them, and re-layouts  1.32 us (2%)
    pallas_call x1, Pallas kernels, body(): pl.pallas_call(functools.partial(kernel, n_mp, n_seq, heads, rows, groups...  78.8 us

profile of v2, /device:TPU:19, one launch (start us, length us, event | category | flops | bytes accessed | tf_op | source)
XLA Modules:
  0.0 80.2 jit_solution(14128836085958487417)
XLA Ops:
  0.0 78.8 %shard_map.82 = bf16[512,2048]{1,0:T(8,128)(2,1)S(1)} custom-call(bf16[2048,512]{1,0:T(8,128)(2,1)} %tokens.1, bf16[2048,512]{1,0:T(8,128)(2,1)} %wq.1, bf16[2048,512]{1,0:T(8,128)(2,1)} %wk.1, bf16[2048,512]{1,0:T(8,128)(2,1)} %wv.1, bf16[2048,512]{1,0:T(8,128)(2,1)} %wg.1, s32[1,4]{1,0:T(1,128)} %bitcast.5, f32[4,2048]{1,0:T(4,128)} %bitcast.3, ...), custom_call_target="tpu_custom_call" | custom-call | tf_op jit(solution)/shard_map/pallas_call | solution.py:434
  78.8 1.3 %copy.10 = bf16[512,2048]{1,0:T(8,128)(2,1)} copy(bf16[512,2048]{1,0:T(8,128)(2,1)S(1)} %shard_map.82) | data formatting | bytes 4194304

commit v3 on v1

--- a/solution.py
+++ b/solution.py
@@ -20,9 +20,9 @@
 def kernel(
     n_mp, n_seq, heads, rows, groups,
     tokens, wq, wk, wv, wg, exponent_in, forget_in, gain_in, out,
-    x, w, exponent, forget, gain, partial, local_out, q_in, gates, moved, got, sq_out, sq_got,
-    state, held, enter, state_out, state_got, offset,
-    weight_sem, small_sem, own_sem, y_send, y_recv, d_send, d_recv, s_send, s_recv, m_send, m_recv, q_send, q_recv,
+    x, w, exponent, forget, gain, decays, summed, by_rows, partial, local_out, q_in, gates, moved, got, sq_out, sq_got,
+    state, held, enter, state_out, state_got, offset, hop_in, hop_out,
+    weight_sem, small_sem, own_sem, y_send, y_recv, d_send, d_recv, s_send, s_recv, m_send, m_recv, q_send, q_recv, hop_send, hop_recv,
 ):
     me = lax.axis_index("mp")
     place = lax.axis_index("seq")
@@ -36,6 +36,10 @@
     head_width = width // heads
     group_heads = heads // groups
     group_width = width // groups
+    ahead = partial.shape[0]
+    relay = n_seq == 2 and chips == 2
+    hop_chunk = 3 if chunks > 4 else chunks - 1
+    across = [lax.rem(chip + 1, chips) * 2 + core, lax.rem(chip + 1, chips) * 2 + (1 - core)]
 
     barrier = pltpu.get_barrier_semaphore()
     for other in range(1, n_mp):
@@ -48,6 +52,10 @@
     @pl.when(place < n_seq - 1)
     def _():
         pl.semaphore_signal(barrier, inc=1, device_id={"seq": place + 1}, device_id_type=MESH)
+
+    if relay:
+        for there in across:
+            pl.semaphore_signal(barrier, inc=1, device_id={"mp": there, "seq": 1 - place}, device_id_type=MESH)
 
     weights = [pltpu.make_async_copy(src, w.at[i], weight_sem.at[i]) for i, src in enumerate((wk, wv, wq, wg))]
     small = [
@@ -98,6 +106,30 @@
         return pltpu.make_async_remote_copy(
             src_ref=there, dst_ref=there, send_sem=d_send.at[c, step], recv_sem=d_recv.at[c, step],
             device_id={"mp": partner}, device_id_type=MESH)
+
+    def in_hop():
+        return pltpu.make_async_remote_copy(
+            src_ref=tokens.at[at_rows(hop_chunk), :], dst_ref=hop_in,
+            send_sem=y_send.at[hop_chunk, 1], recv_sem=hop_recv.at[2],
+            device_id={"mp": across[0], "seq": 1}, device_id_type=MESH)
+
+    def in_next():
+        return pltpu.make_async_remote_copy(
+            src_ref=hop_in, dst_ref=x.at[at_rows(hop_chunk), columns(across[0])],
+            send_sem=hop_send.at[2], recv_sem=y_recv.at[hop_chunk, 1],
+            device_id={"seq": 0}, device_id_type=MESH)
+
+    def out_hop(block, to, i):
+        return pltpu.make_async_remote_copy(
+            src_ref=moved.at[at_rows(block), pl.ds(0, group_width)], dst_ref=hop_out.at[i],
+            send_sem=m_send.at[block, 0], recv_sem=hop_recv.at[i],
+            device_id={"mp": to, "seq": 0}, device_id_type=MESH)
+
+    def out_next(i):
+        return pltpu.make_async_remote_copy(
+            src_ref=hop_out.at[i], dst_ref=got.at[across[i], at_rows(0), pl.ds(0, group_width)],
+            send_sem=hop_send.at[i], recv_sem=m_recv.at[across[i], 0, 0],
+            device_id={"seq": 1}, device_id_type=MESH)
 
     for copy in small:
         copy.start()
@@ -107,12 +139,18 @@
     pl.loop(1, chunks)(lambda c: own_copy(c).start())
 
     neighbours = jnp.minimum(place, 1) + jnp.minimum(n_seq - 1 - place, 1)
-    pl.semaphore_wait(barrier, n_mp - 1 + neighbours)
+    pl.semaphore_wait(barrier, n_mp - 1 + neighbours + (2 if relay else 0))
+
+    if relay:
+        pl.when(place == 0)(lambda: in_hop().start())
 
     @pl.loop(0, chunks)
     def _(c):
         for step in range(1, chips):
-            y_copy(c, step).start()
+            if relay:
+                pl.when(jnp.logical_or(place > 0, c != hop_chunk))(lambda: y_copy(c, step).start())
+            else:
+                y_copy(c, step).start()
         d_copy(c, 0).start()
 
     state[...] = jnp.zeros_like(state)
@@ -132,8 +170,26 @@
     diagonal = lax.broadcasted_iota(jnp.int32, (heads, heads), 0) == lax.broadcasted_iota(jnp.int32, (heads, heads), 1)
     column = jnp.sum(jnp.where(diagonal, spread, 0.0), axis=1, keepdims=True)
     rate = jnp.log1p(-jnp.exp2(-column))
+    for c in range(chunks):
+        decays[c * heads : (c + 1) * heads, :] = rate - forget[:, c * rows : (c + 1) * rows]
+    every = jnp.dot(decays[...], summing, precision=exact, preferred_element_type=F32)
+    turned = every.T
+    for c in range(chunks):
+        summed[c] = every[c * heads : (c + 1) * heads, :]
+        by_rows[c] = turned[:, c * heads : (c + 1) * heads]
+
+    def near(c):
+        own_copy(c).wait()
+        d_arrival(c, 0).wait_recv()
+        own_side = pl.ds(pl.multiple_of(chip * 2 * width, 2 * width), 2 * width)
+        piece = x[at_rows(c), own_side]
+        slot = lax.rem(c, ahead)
+        for i in range(4):
+            partial[slot, i] = jnp.dot(piece, w[i, own_side, :], preferred_element_type=F32)
+
     for copy in weights:
         copy.wait()
+    pl.loop(0, ahead)(near)
 
     def s_copy(g):
         part = pl.ds(g * group_heads, group_heads)
@@ -161,17 +217,16 @@
     def finalize(block, g):
         here = at_rows(block)
         to, r = block // parts, lax.rem(block, parts)
-        squares = jnp.zeros((8, rows), F32)
+        square = jnp.zeros((rows, head_width), F32)
         for h in range(g * group_heads, (g + 1) * group_heads):
             part = slice(h * head_width, (h + 1) * head_width)
             whole = local_out[here, part] + jnp.dot(q_in[here, part], enter[h], preferred_element_type=F32)
             kept = whole.astype(BF16).astype(F32)
             moved[here, part] = (gates[here, part] * kept).astype(BF16)
-            square = kept * kept
-            high = square.astype(BF16)
-            low = (square - high.astype(F32)).astype(BF16)
-            squares += contract(ones, high, ((1,), (1,))) + contract(ones, low, ((1,), (1,)))
-        total = squares[0:1, :]
+            square += kept * kept
+        high = square.astype(BF16)
+        low = (square - high.astype(F32)).astype(BF16)
+        total = (contract(ones, high, ((1,), (1,))) + contract(ones, low, ((1,), (1,))))[0:1, :]
         if g > 0:
             total = total + sq_out[block]
         sq_out[block] = total
@@ -180,7 +235,12 @@
         def _():
             if g == groups - 1:
                 q_copy(block).start()
-            m_copy(block, g).start()
+            if relay and g == 0:
+                detour = jnp.logical_and(jnp.logical_and(place == 1, r == 0), to // 2 != chip)
+                pl.when(detour)(lambda: out_hop(block, to, lax.rem(core + to, 2)).start())
+                pl.when(jnp.logical_not(detour))(lambda: m_copy(block, g).start())
+            else:
+                m_copy(block, g).start()
 
         @pl.when(to == me)
         def _():
@@ -189,34 +249,71 @@
             if g == groups - 1:
                 sq_got[me, r] = total
 
+    far_steps = (n_mp - 2) * parts
+
+    def away(step):
+        o = lax.rem(step, n_mp - 2)
+        return (lax.rem(chip + o // 2 + 1, chips) * 2 + lax.rem(core + o, 2)) * parts + step // (n_mp - 2)
+
+    def home(step):
+        return (chip * 2 + lax.rem(core + 1 + step, 2)) * parts + step // 2
+
+    def enter_state(g):
+        part = slice(g * group_heads, (g + 1) * group_heads)
+        s_copy(g).wait_recv()
+        enter[part] = state_got[part]
+
+    def ready_far(g, low, high):
+        @pl.loop(0, far_steps)
+        def _(step):
+            block = away(lax.rem(step + 2, far_steps))
+            pl.when(jnp.logical_and(block >= low, block < high))(lambda: finalize(block, g))
+
     @pl.loop(0, chunks)
     def _(c):
         here = at_rows(c)
-        decay = rate - forget[:, here]
-        running = jnp.dot(decay, summing, precision=exact, preferred_element_type=F32)
-        by_row = lax.dot_general(
-            causal.astype(F32), decay, (((1,), (1,)), ((), ())), precision=exact, preferred_element_type=F32)
+        slot = lax.rem(c, ahead)
+        running, by_row = summed[c], by_rows[c]
         last = running[:, rows - 1 :]
         before = offset[...]
 
-        own_copy(c).wait()
-        d_arrival(c, 0).wait_recv()
-        own_side = pl.ds(pl.multiple_of(chip * 2 * width, 2 * width), 2 * width)
-        piece = x[here, own_side]
-        for i in range(4):
-            partial[i] = jnp.dot(piece, w[i, own_side, :], preferred_element_type=F32)
+        if relay:
+            @pl.when(jnp.logical_and(place == 1, c == 1))
+            def _():
+                in_hop().wait_recv()
+                in_next().start()
+
+            @pl.when(jnp.logical_and(place == 1, c == chunks - 1))
+            def _():
+                ready_far(0, chunks - 2, chunks - 1)
+                for g in range(1, groups):
+                    enter_state(g)
+                    ready_far(g, 0, chunks - 1)
+
         for step in range(1, chips):
             y_arrival(c, step).wait_recv()
             d_copy(c, step).start()
         for step in range(1, chips):
             piece = x[here, columns(back(step))]
             for i in range(4):
-                partial[i] += jnp.dot(piece, w[i, columns(back(step)), :], preferred_element_type=F32)
+                partial[slot, i] += jnp.dot(piece, w[i, columns(back(step)), :], preferred_element_type=F32)
+
+        @pl.when(jnp.logical_and(place == 0, c > 0))
+        def _():
+            for g in range(groups):
+                finalize(c - 1, g)
+
         for step in range(1, chips):
             d_arrival(c, step).wait_recv()
 
+        if relay:
+            @pl.when(jnp.logical_and(place == 1, c == chunks - 2))
+            def _():
+                enter_state(0)
+                ready_far(0, 0, chunks - 2)
+
         def project(i):
-            total = partial[i]
+            total = partial[slot, i]
             for step in range(1, chips):
                 total += jnp.dot(
                     x[here, columns(back_other(step))], w[i, columns(back_other(step)), :],
@@ -256,27 +353,21 @@
         gate = project(3).astype(BF16).astype(F32)
         gates[here, :] = gate / (1.0 + jnp.exp(-gate))
 
-        @pl.when(place == 0)
-        def _():
-            for g in range(groups):
-                finalize(c, g)
-
-    far_steps = (n_mp - 2) * parts
-
-    def in_order(step):
-        o = lax.rem(step, n_mp - 2)
-        away = (lax.rem(chip + o // 2 + 1, chips) * 2 + lax.rem(core + o, 2)) * parts + step // (n_mp - 2)
-        rest = jnp.maximum(step - far_steps, 0)
-        home = (chip * 2 + lax.rem(core + 1 + rest, 2)) * parts + rest // 2
-        return jnp.where(step < far_steps, away, home)
+        pl.when(c < chunks - ahead)(lambda: near(c + ahead))
+
+    @pl.when(place == 0)
+    def _():
+        for g in range(groups):
+            finalize(chunks - 1, g)
 
     if n_seq > 1:
         @pl.when(place > 0)
         def _():
             for g in range(groups):
-                part = slice(g * group_heads, (g + 1) * group_heads)
-                s_copy(g).wait_recv()
-                enter[part] = state_got[part]
+                if relay:
+                    pl.when((chunks - 1) // parts // 2 != chip)(lambda: finalize(chunks - 1, g))
+                    continue
+                enter_state(g)
                 if n_seq > 2:
                     @pl.when(place < n_seq - 1)
                     def _():
@@ -285,7 +376,19 @@
                             state_out[h] = (total * enter[h].astype(F32) + state[h]).astype(BF16)
                         s_copy(g).start()
 
-                pl.loop(0, chunks)(lambda step: finalize(in_order(step), g))
+                pl.loop(0, far_steps)(lambda step: finalize(away(step), g))
+
+            @pl.loop(0, 2 * parts)
+            def _(step):
+                for g in range(groups):
+                    finalize(home(step), g)
+
+    if relay:
+        @pl.when(place == 0)
+        def _():
+            for i in range(2):
+                out_hop(0, across[i], i).wait_recv()
+                out_next(i).start()
 
     def m_arrival(source, r, g):
         there = got.at[source, at_rows(r), group_columns(g)]
@@ -337,6 +440,18 @@
             for g in range(groups):
                 s_copy(g).wait_send()
 
+    if relay:
+        @pl.when(place == 0)
+        def _():
+            for i in range(2):
+                out_next(i).wait_send()
+
+        pl.when(place == 1)(lambda: in_next().wait_send())
+
+
+def in_hbm(a):
+    return a if a.size == 1 else pltpu.with_memory_space_constraint(a, pltpu.HBM)
+
 
 def body(n_mp, n_seq, tokens, w_query, w_key, w_value, w_gate, decay_exponent, forget, norm_gain):
     seq_rows, width = tokens.shape
@@ -346,7 +461,7 @@
     rows = 256 if own_rows % 256 == 0 else own_rows
     chunks, parts = seq_rows // rows, own_rows // rows
     groups = 2 if heads % 2 == 0 else 1
-    hbm = pl.BlockSpec(memory_space=pl.ANY)
+    hbm = pl.BlockSpec(memory_space=pltpu.HBM)
     dma = pltpu.SemaphoreType.DMA
     chips = n_mp // 2
     return pl.pallas_call(
@@ -360,7 +475,10 @@
             pltpu.VMEM((1, heads), jnp.int32),
             pltpu.VMEM((heads, seq_rows), F32),
             pltpu.VMEM((1, features), F32),
-            pltpu.VMEM((4, rows, width), F32),
+            pltpu.VMEM((chunks * heads, rows), F32),
+            pltpu.VMEM((chunks, heads, rows), F32),
+            pltpu.VMEM((chunks, rows, heads), F32),
+            pltpu.VMEM((4, 4, rows, width), F32),
             pltpu.VMEM((seq_rows, width), F32),
             pltpu.VMEM((seq_rows, width), BF16),
             pltpu.VMEM((seq_rows, width), F32),
@@ -374,6 +492,8 @@
             pltpu.VMEM((heads, DH, DH), BF16),
             pltpu.VMEM((heads, DH, DH), BF16),
             pltpu.VMEM((heads, 128), F32),
+            pltpu.VMEM((rows, width), BF16),
+            pltpu.VMEM((2, rows, width // groups), BF16),
             dma((4,)),
             dma((3,)),
             dma((chunks,)),
@@ -387,11 +507,13 @@
             dma((n_mp, parts, groups)),
             dma((chunks,)),
             dma((n_mp, parts)),
+            dma((3,)),
+            dma((3,)),
         ],
         compiler_params=pltpu.CompilerParams(
-            collective_id=0, has_side_effects=True, vmem_limit_bytes=48 * 1024 * 1024
+            collective_id=0, has_side_effects=True, vmem_limit_bytes=56 * 1024 * 1024
         ),
-    )(tokens, w_query, w_key, w_value, w_gate, decay_exponent[None, :], forget.T, norm_gain[None, :])
+    )(*(in_hbm(a) for a in (tokens, w_query, w_key, w_value, w_gate, decay_exponent[None, :], forget.T, norm_gain[None, :])))
 
 
 def solution(mesh):

time: 85.4 us -> 75.3 us (0.88); the launches traced: 85.2 us -> 73.9 us
  Pallas kernels: 80.1 us -> 72.6 us
  local copies, waits for them, and re-layouts: 5.02 us -> 1.32 us
    pallas_call x1, Pallas kernels: 80.1 us -> 72.6 us  [body(): pl.pallas_call(functools.partial(kernel, n_mp, n_seq, heads, rows, groups...]
    unnamed x9 -> x1, local copies, waits for them, and re-layouts: 5.02 us -> 1.32 us
where the time goes in v3:
time: 75.3 us; the launch traced here: 73.9 us
  Pallas kernels  72.6 us (96%)
  local copies, waits for them, and re-layouts  1.32 us (2%)
    pallas_call x1, Pallas kernels, body(): pl.pallas_call(functools.partial(kernel, n_mp, n_seq, heads, rows, groups...  72.6 us

profile of v3, /device:TPU:19, one launch (start us, length us, event | category | flops | bytes accessed | tf_op | source)
XLA Modules:
  0.0 73.9 jit_solution(6249517253477562581)
XLA Ops:
  0.0 72.6 %shard_map.82 = bf16[512,2048]{1,0:T(8,128)(2,1)S(1)} custom-call(bf16[2048,512]{1,0:T(8,128)(2,1)} %tokens.1, bf16[2048,512]{1,0:T(8,128)(2,1)} %wq.1, bf16[2048,512]{1,0:T(8,128)(2,1)} %wk.1, bf16[2048,512]{1,0:T(8,128)(2,1)} %wv.1, bf16[2048,512]{1,0:T(8,128)(2,1)} %wg.1, s32[1,4]{1,0:T(1,128)} %bitcast.5, f32[4,2048]{1,0:T(4,128)} %bitcast.3, ...), custom_call_target="tpu_custom_call" | custom-call | tf_op jit(solution)/shard_map/pallas_call | solution.py:467
  72.6 1.3 %copy.10 = bf16[512,2048]{1,0:T(8,128)(2,1)} copy(bf16[512,2048]{1,0:T(8,128)(2,1)S(1)} %shard_map.82) | data formatting | bytes 4194304

commit v4 on v3

--- a/solution.py
+++ b/solution.py
@@ -22,7 +22,7 @@
     tokens, wq, wk, wv, wg, exponent_in, forget_in, gain_in, out,
     x, w, exponent, forget, gain, decays, summed, by_rows, partial, local_out, q_in, gates, moved, got, sq_out, sq_got,
     state, held, enter, state_out, state_got, offset, hop_in, hop_out,
-    weight_sem, small_sem, own_sem, y_send, y_recv, d_send, d_recv, s_send, s_recv, m_send, m_recv, q_send, q_recv, hop_send, hop_recv,
+    weight_sem, small_sem, own_sem, y_send, y_recv, p_send, p_recv, d_send, d_recv, s_send, s_recv, m_send, m_recv, q_send, q_recv, hop_send, hop_recv,
 ):
     me = lax.axis_index("mp")
     place = lax.axis_index("seq")
@@ -57,7 +57,7 @@
         for there in across:
             pl.semaphore_signal(barrier, inc=1, device_id={"mp": there, "seq": 1 - place}, device_id_type=MESH)
 
-    weights = [pltpu.make_async_copy(src, w.at[i], weight_sem.at[i]) for i, src in enumerate((wk, wv, wq, wg))]
+    weights = [pltpu.make_async_copy(src, w.at[i], weight_sem) for i, src in enumerate((wk, wv, wq, wg))]
     small = [
         pltpu.make_async_copy(src, dst, small_sem.at[i])
         for i, (src, dst) in enumerate(((exponent_in, exponent), (forget_in, forget), (gain_in, gain)))
@@ -69,8 +69,8 @@
     def at_rows(c):
         return pl.ds(pl.multiple_of(c * rows, rows), rows)
 
-    def own_copy(c):
-        return pltpu.make_async_copy(tokens.at[at_rows(c), :], x.at[at_rows(c), columns(me)], own_sem.at[c])
+    def own_copy():
+        return pltpu.make_async_copy(tokens, x.at[:, columns(me)], own_sem)
 
     def far(step):
         return lax.rem(chip + step, chips) * 2 + core
@@ -84,59 +84,71 @@
     def y_copy(c, step):
         return pltpu.make_async_remote_copy(
             src_ref=tokens.at[at_rows(c), :], dst_ref=x.at[at_rows(c), columns(me)],
-            send_sem=y_send.at[c, step], recv_sem=y_recv.at[c, step],
+            send_sem=y_send.at[step - 1], recv_sem=y_recv.at[c, step - 1],
             device_id={"mp": far(step)}, device_id_type=MESH)
 
     def y_arrival(c, step):
         return pltpu.make_async_remote_copy(
             src_ref=tokens.at[at_rows(c), :], dst_ref=x.at[at_rows(c), columns(back(step))],
-            send_sem=y_send.at[c, step], recv_sem=y_recv.at[c, step],
+            send_sem=y_send.at[step - 1], recv_sem=y_recv.at[c, step - 1],
             device_id={"mp": far(step)}, device_id_type=MESH)
 
+    def at_pair(i):
+        return pl.ds(pl.multiple_of(i * 2 * rows, 2 * rows), 2 * rows)
+
+    def p_copy(i):
+        return pltpu.make_async_remote_copy(
+            src_ref=tokens.at[at_pair(i), :], dst_ref=x.at[at_pair(i), columns(me)],
+            send_sem=p_send, recv_sem=p_recv.at[i],
+            device_id={"mp": partner}, device_id_type=MESH)
+
+    def p_arrival(i):
+        there = x.at[at_pair(i), columns(partner)]
+        return pltpu.make_async_remote_copy(
+            src_ref=there, dst_ref=there, send_sem=p_send, recv_sem=p_recv.at[i],
+            device_id={"mp": partner}, device_id_type=MESH)
+
     def d_copy(c, step):
-        block = me if step == 0 else back(step)
-        source = tokens.at[at_rows(c), :] if step == 0 else x.at[at_rows(c), columns(block)]
-        return pltpu.make_async_remote_copy(
-            src_ref=source, dst_ref=x.at[at_rows(c), columns(block)],
-            send_sem=d_send.at[c, step], recv_sem=d_recv.at[c, step],
+        there = x.at[at_rows(c), columns(back(step))]
+        return pltpu.make_async_remote_copy(
+            src_ref=there, dst_ref=there, send_sem=d_send.at[step - 1], recv_sem=d_recv.at[c, step - 1],
             device_id={"mp": partner}, device_id_type=MESH)
 
     def d_arrival(c, step):
-        there = x.at[at_rows(c), columns(partner if step == 0 else back_other(step))]
-        return pltpu.make_async_remote_copy(
-            src_ref=there, dst_ref=there, send_sem=d_send.at[c, step], recv_sem=d_recv.at[c, step],
+        there = x.at[at_rows(c), columns(back_other(step))]
+        return pltpu.make_async_remote_copy(
+            src_ref=there, dst_ref=there, send_sem=d_send.at[step - 1], recv_sem=d_recv.at[c, step - 1],
             device_id={"mp": partner}, device_id_type=MESH)
 
     def in_hop():
         return pltpu.make_async_remote_copy(
             src_ref=tokens.at[at_rows(hop_chunk), :], dst_ref=hop_in,
-            send_sem=y_send.at[hop_chunk, 1], recv_sem=hop_recv.at[2],
+            send_sem=y_send.at[0], recv_sem=hop_recv.at[0],
             device_id={"mp": across[0], "seq": 1}, device_id_type=MESH)
 
     def in_next():
         return pltpu.make_async_remote_copy(
             src_ref=hop_in, dst_ref=x.at[at_rows(hop_chunk), columns(across[0])],
-            send_sem=hop_send.at[2], recv_sem=y_recv.at[hop_chunk, 1],
+            send_sem=hop_send, recv_sem=y_recv.at[hop_chunk, 0],
             device_id={"seq": 0}, device_id_type=MESH)
 
     def out_hop(block, to, i):
         return pltpu.make_async_remote_copy(
             src_ref=moved.at[at_rows(block), pl.ds(0, group_width)], dst_ref=hop_out.at[i],
-            send_sem=m_send.at[block, 0], recv_sem=hop_recv.at[i],
+            send_sem=m_send, recv_sem=hop_recv.at[i],
             device_id={"mp": to, "seq": 0}, device_id_type=MESH)
 
     def out_next(i):
         return pltpu.make_async_remote_copy(
             src_ref=hop_out.at[i], dst_ref=got.at[across[i], at_rows(0), pl.ds(0, group_width)],
-            send_sem=hop_send.at[i], recv_sem=m_recv.at[across[i], 0, 0],
+            send_sem=hop_send, recv_sem=m_recv.at[across[i], 0],
             device_id={"seq": 1}, device_id_type=MESH)
 
     for copy in small:
         copy.start()
-    own_copy(0).start()
+    own_copy().start()
     for copy in weights:
         copy.start()
-    pl.loop(1, chunks)(lambda c: own_copy(c).start())
 
     neighbours = jnp.minimum(place, 1) + jnp.minimum(n_seq - 1 - place, 1)
     pl.semaphore_wait(barrier, n_mp - 1 + neighbours + (2 if relay else 0))
@@ -151,7 +163,7 @@
                 pl.when(jnp.logical_or(place > 0, c != hop_chunk))(lambda: y_copy(c, step).start())
             else:
                 y_copy(c, step).start()
-        d_copy(c, 0).start()
+        pl.when(lax.rem(c, 2) == 0)(lambda: p_copy(c // 2).start())
 
     state[...] = jnp.zeros_like(state)
     offset[...] = jnp.zeros_like(offset)
@@ -179,22 +191,21 @@
         by_rows[c] = turned[:, c * heads : (c + 1) * heads]
 
     def near(c):
-        own_copy(c).wait()
-        d_arrival(c, 0).wait_recv()
+        pl.when(lax.rem(c, 2) == 0)(lambda: p_arrival(c // 2).wait_recv())
         own_side = pl.ds(pl.multiple_of(chip * 2 * width, 2 * width), 2 * width)
         piece = x[at_rows(c), own_side]
         slot = lax.rem(c, ahead)
         for i in range(4):
             partial[slot, i] = jnp.dot(piece, w[i, own_side, :], preferred_element_type=F32)
 
-    for copy in weights:
-        copy.wait()
+    own_copy().wait()
+    pltpu.make_async_copy(w, w, weight_sem).wait()
     pl.loop(0, ahead)(near)
 
     def s_copy(g):
         part = pl.ds(g * group_heads, group_heads)
         return pltpu.make_async_remote_copy(
-            src_ref=state_out.at[part], dst_ref=state_got.at[part], send_sem=s_send.at[g], recv_sem=s_recv.at[g],
+            src_ref=state_out.at[part], dst_ref=state_got.at[part], send_sem=s_send, recv_sem=s_recv.at[g],
             device_id={"seq": lax.rem(place + 1, n_seq)}, device_id_type=MESH)
 
     def group_columns(g):
@@ -204,14 +215,14 @@
         to, r = block // parts, lax.rem(block, parts)
         return pltpu.make_async_remote_copy(
             src_ref=moved.at[at_rows(block), group_columns(g)], dst_ref=got.at[me, at_rows(r), group_columns(g)],
-            send_sem=m_send.at[block, g], recv_sem=m_recv.at[me, r, g],
+            send_sem=m_send, recv_sem=m_recv.at[me, r],
             device_id={"mp": to}, device_id_type=MESH)
 
     def q_copy(block):
         to, r = block // parts, lax.rem(block, parts)
         return pltpu.make_async_remote_copy(
-            src_ref=sq_out.at[block], dst_ref=sq_got.at[me, r],
-            send_sem=q_send.at[block], recv_sem=q_recv.at[me, r],
+            src_ref=sq_out.at[block], dst_ref=sq_got.at[r, me],
+            send_sem=q_send, recv_sem=q_recv.at[r],
             device_id={"mp": to}, device_id_type=MESH)
 
     def finalize(block, g):
@@ -247,7 +258,7 @@
             part = slice(g * group_width, (g + 1) * group_width)
             got[me, at_rows(r), part] = moved[here, part]
             if g == groups - 1:
-                sq_got[me, r] = total
+                sq_got[r, me] = total
 
     far_steps = (n_mp - 2) * parts
 
@@ -390,63 +401,49 @@
                 out_hop(0, across[i], i).wait_recv()
                 out_next(i).start()
 
-    def m_arrival(source, r, g):
-        there = got.at[source, at_rows(r), group_columns(g)]
-        return pltpu.make_async_remote_copy(
-            src_ref=there, dst_ref=there, send_sem=m_send.at[0, 0], recv_sem=m_recv.at[source, r, g],
+    def m_arrival(source, r):
+        there = got.at[source, at_rows(r), :]
+        return pltpu.make_async_remote_copy(
+            src_ref=there, dst_ref=there, send_sem=m_send, recv_sem=m_recv.at[source, r],
             device_id={"mp": partner}, device_id_type=MESH)
 
-    def q_arrival(source, r):
-        there = sq_got.at[source, r]
-        return pltpu.make_async_remote_copy(
-            src_ref=there, dst_ref=there, send_sem=q_send.at[0], recv_sem=q_recv.at[source, r],
+    def q_arrival(r):
+        there = sq_got.at[r, pl.ds(0, n_mp - 1)]
+        return pltpu.make_async_remote_copy(
+            src_ref=there, dst_ref=there, send_sem=q_send, recv_sem=q_recv.at[r],
             device_id={"mp": partner}, device_id_type=MESH)
 
     sources = [me, partner] + [lax.rem(chip + t, chips) * 2 + lax.rem(core + s, 2) for t in range(1, chips) for s in (0, 1)]
 
     for r in range(parts):
-        for source in sources[1:]:
-            q_arrival(source, r).wait_recv()
-        total = sq_got[0, r]
+        q_arrival(r).wait_recv()
+        total = sq_got[r, 0]
         for source in range(1, n_mp):
-            total += sq_got[source, r]
+            total += sq_got[r, source]
         scale = lax.rsqrt(total * (1.0 / (n_mp * width)) + 1e-06)
         scale = jnp.broadcast_to(scale, (8, rows)).T[:, 0:1]
         span = slice(r * rows, (r + 1) * rows)
-        for g in range(groups):
-            for i, source in enumerate(sources):
-                if i > 0:
-                    m_arrival(source, r, g).wait_recv()
-                part = pl.ds(pl.multiple_of(source * width + g * group_width, group_width), group_width)
-                piece = got[source, span, g * group_width : (g + 1) * group_width].astype(F32)
-                out[span, part] = (piece * scale * gain[:, part]).astype(BF16)
-
-    @pl.loop(0, chunks)
-    def _(c):
-        for step in range(1, chips):
-            y_copy(c, step).wait_send()
-        for step in range(chips):
-            d_copy(c, step).wait_send()
-
-        @pl.when(c // parts != me)
-        def _():
-            q_copy(c).wait_send()
-            for g in range(groups):
-                m_copy(c, g).wait_send()
-
+        for i, source in enumerate(sources):
+            if i > 0:
+                m_arrival(source, r).wait_recv()
+            out[span, columns(source)] = (got[source, span, :].astype(F32) * scale * gain[:, columns(source)]).astype(BF16)
+
+    def sent(ref, sem):
+        pltpu.make_async_remote_copy(
+            src_ref=ref, dst_ref=ref, send_sem=sem, recv_sem=own_sem,
+            device_id={"mp": partner}, device_id_type=MESH).wait_send()
+
+    for step in range(1, chips):
+        sent(tokens, y_send.at[step - 1])
+        sent(x.at[:, columns(0)], d_send.at[step - 1])
+    sent(tokens, p_send)
+    sent(sq_out.at[pl.ds(0, chunks - parts)], q_send)
+    sent(moved.at[pl.ds(0, seq_rows - own_rows), :], m_send)
     if n_seq > 1:
-        @pl.when(place < n_seq - 1)
-        def _():
-            for g in range(groups):
-                s_copy(g).wait_send()
-
+        pl.when(place < n_seq - 1)(lambda: sent(state_out, s_send))
     if relay:
-        @pl.when(place == 0)
-        def _():
-            for i in range(2):
-                out_next(i).wait_send()
-
-        pl.when(place == 1)(lambda: in_next().wait_send())
+        pl.when(place == 0)(lambda: sent(hop_out, hop_send))
+        pl.when(place == 1)(lambda: sent(hop_in, hop_send))
 
 
 def in_hbm(a):
@@ -485,7 +482,7 @@
             pltpu.VMEM((seq_rows, width), BF16),
             pltpu.VMEM((n_mp, own_rows, width), BF16),
             pltpu.VMEM((chunks, 1, rows), F32),
-            pltpu.VMEM((n_mp, parts, 1, rows), F32),
+            pltpu.VMEM((parts, n_mp, 1, rows), F32),
             pltpu.VMEM((heads, DH, DH), F32),
             pltpu.VMEM((heads, DH, DH), BF16),
             pltpu.VMEM((heads, DH, DH), BF16),
@@ -494,21 +491,23 @@
             pltpu.VMEM((heads, 128), F32),
             pltpu.VMEM((rows, width), BF16),
             pltpu.VMEM((2, rows, width // groups), BF16),
-            dma((4,)),
+            dma,
             dma((3,)),
-            dma((chunks,)),
-            dma((chunks, chips)),
-            dma((chunks, chips)),
-            dma((chunks, chips)),
-            dma((chunks, chips)),
+            dma,
+            dma((chips - 1,)),
+            dma((chunks, chips - 1)),
+            dma,
+            dma((chunks // 2,)),
+            dma((chips - 1,)),
+            dma((chunks, chips - 1)),
+            dma,
             dma((groups,)),
-            dma((groups,)),
-            dma((chunks, groups)),
-            dma((n_mp, parts, groups)),
-            dma((chunks,)),
+            dma,
             dma((n_mp, parts)),
-            dma((3,)),
-            dma((3,)),
+            dma,
+            dma((parts,)),
+            dma,
+            dma((2,)),
         ],
         compiler_params=pltpu.CompilerParams(
             collective_id=0, has_side_effects=True, vmem_limit_bytes=56 * 1024 * 1024

time: 75.3 us -> 74.4 us (0.988)
  Pallas kernels: 72.6 us -> 71.6 us
    pallas_call x1, Pallas kernels: 72.6 us -> 71.6 us  [body(): pl.pallas_call(functools.partial(kernel, n_mp, n_seq, heads, rows, groups...]
where the time goes in v4:
time: 74.4 us; the launch traced here: 73 us
  Pallas kernels  71.6 us (96%)
  local copies, waits for them, and re-layouts  1.32 us (2%)
    pallas_call x1, Pallas kernels, body(): pl.pallas_call(functools.partial(kernel, n_mp, n_seq, heads, rows, groups...  71.6 us

profile of v4, /device:TPU:19, one launch (start us, length us, event | category | flops | bytes accessed | tf_op | source)
XLA Modules:
  0.0 73.0 jit_solution(16288649435438337011)
XLA Ops:
  0.0 71.6 %shard_map.82 = bf16[512,2048]{1,0:T(8,128)(2,1)S(1)} custom-call(bf16[2048,512]{1,0:T(8,128)(2,1)} %tokens.1, bf16[2048,512]{1,0:T(8,128)(2,1)} %wq.1, bf16[2048,512]{1,0:T(8,128)(2,1)} %wk.1, bf16[2048,512]{1,0:T(8,128)(2,1)} %wv.1, bf16[2048,512]{1,0:T(8,128)(2,1)} %wg.1, s32[1,4]{1,0:T(1,128)} %bitcast.5, f32[4,2048]{1,0:T(4,128)} %bitcast.3, ...), custom_call_target="tpu_custom_call" | custom-call | tf_op jit(solution)/shard_map/pallas_call | solution.py:464
  71.7 1.3 %copy.10 = bf16[512,2048]{1,0:T(8,128)(2,1)} copy(bf16[512,2048]{1,0:T(8,128)(2,1)S(1)} %shard_map.82) | data formatting | bytes 4194304

commit v5 on v4

--- a/solution.py
+++ b/solution.py
@@ -22,7 +22,7 @@
     tokens, wq, wk, wv, wg, exponent_in, forget_in, gain_in, out,
     x, w, exponent, forget, gain, decays, summed, by_rows, partial, local_out, q_in, gates, moved, got, sq_out, sq_got,
     state, held, enter, state_out, state_got, offset, hop_in, hop_out,
-    weight_sem, small_sem, own_sem, y_send, y_recv, p_send, p_recv, d_send, d_recv, s_send, s_recv, m_send, m_recv, q_send, q_recv, hop_send, hop_recv,
+    weight_sem, small_sem, own_sem, y_send, y_recv, p_send, p_recv, d_send, d_recv, s_send, s_recv, m_send, m_recv, q_send, q_recv, hop_send, hop_recv, ready,
 ):
     me = lax.axis_index("mp")
     place = lax.axis_index("seq")
@@ -45,17 +45,21 @@
     for other in range(1, n_mp):
         pl.semaphore_signal(barrier, inc=1, device_id={"mp": lax.rem(me + other, n_mp)}, device_id_type=MESH)
 
-    @pl.when(place > 0)
-    def _():
-        pl.semaphore_signal(barrier, inc=1, device_id={"seq": place - 1}, device_id_type=MESH)
-
-    @pl.when(place < n_seq - 1)
-    def _():
-        pl.semaphore_signal(barrier, inc=1, device_id={"seq": place + 1}, device_id_type=MESH)
+    across_place = [{"seq": 1 - place}] + [{"mp": there, "seq": 1 - place} for there in across]
 
     if relay:
-        for there in across:
-            pl.semaphore_signal(barrier, inc=1, device_id={"mp": there, "seq": 1 - place}, device_id_type=MESH)
+        @pl.when(place == 0)
+        def _():
+            for there in across_place:
+                pl.semaphore_signal(barrier, inc=1, device_id=there, device_id_type=MESH)
+    else:
+        @pl.when(place > 0)
+        def _():
+            pl.semaphore_signal(barrier, inc=1, device_id={"seq": place - 1}, device_id_type=MESH)
+
+        @pl.when(place < n_seq - 1)
+        def _():
+            pl.semaphore_signal(barrier, inc=1, device_id={"seq": place + 1}, device_id_type=MESH)
 
     weights = [pltpu.make_async_copy(src, w.at[i], weight_sem) for i, src in enumerate((wk, wv, wq, wg))]
     small = [
@@ -132,15 +136,24 @@
             send_sem=hop_send, recv_sem=y_recv.at[hop_chunk, 0],
             device_id={"seq": 0}, device_id_type=MESH)
 
+    hop_rows = hop_out.shape[1]
+
     def out_hop(block, to, i):
         return pltpu.make_async_remote_copy(
-            src_ref=moved.at[at_rows(block), pl.ds(0, group_width)], dst_ref=hop_out.at[i],
-            send_sem=m_send, recv_sem=hop_recv.at[i],
+            src_ref=moved.at[pl.ds(pl.multiple_of(block * rows, rows), hop_rows), pl.ds(0, group_width)],
+            dst_ref=hop_out.at[i], send_sem=m_send, recv_sem=hop_recv.at[i],
             device_id={"mp": to, "seq": 0}, device_id_type=MESH)
 
+    def out_rest(block, to):
+        left = rows - hop_rows
+        return pltpu.make_async_remote_copy(
+            src_ref=moved.at[pl.ds(pl.multiple_of(block * rows + hop_rows, left), left), pl.ds(0, group_width)],
+            dst_ref=got.at[me, pl.ds(hop_rows, left), pl.ds(0, group_width)],
+            send_sem=m_send, recv_sem=m_recv.at[me, 0], device_id={"mp": to}, device_id_type=MESH)
+
     def out_next(i):
         return pltpu.make_async_remote_copy(
-            src_ref=hop_out.at[i], dst_ref=got.at[across[i], at_rows(0), pl.ds(0, group_width)],
+            src_ref=hop_out.at[i], dst_ref=got.at[across[i], pl.ds(0, hop_rows), pl.ds(0, group_width)],
             send_sem=hop_send, recv_sem=m_recv.at[across[i], 0],
             device_id={"seq": 1}, device_id_type=MESH)
 
@@ -150,11 +163,11 @@
     for copy in weights:
         copy.start()
 
-    neighbours = jnp.minimum(place, 1) + jnp.minimum(n_seq - 1 - place, 1)
-    pl.semaphore_wait(barrier, n_mp - 1 + neighbours + (2 if relay else 0))
-
     if relay:
-        pl.when(place == 0)(lambda: in_hop().start())
+        neighbours = place * len(across_place)
+    else:
+        neighbours = jnp.minimum(place, 1) + jnp.minimum(n_seq - 1 - place, 1)
+    pl.semaphore_wait(barrier, n_mp - 1 + neighbours)
 
     @pl.loop(0, chunks)
     def _(c):
@@ -164,6 +177,12 @@
             else:
                 y_copy(c, step).start()
         pl.when(lax.rem(c, 2) == 0)(lambda: p_copy(c // 2).start())
+
+    if relay:
+        @pl.when(place == 1)
+        def _():
+            for there in across_place:
+                pl.semaphore_signal(ready, inc=1, device_id=there, device_id_type=MESH)
 
     state[...] = jnp.zeros_like(state)
     offset[...] = jnp.zeros_like(offset)
@@ -197,6 +216,12 @@
         slot = lax.rem(c, ahead)
         for i in range(4):
             partial[slot, i] = jnp.dot(piece, w[i, own_side, :], preferred_element_type=F32)
+
+    if relay:
+        @pl.when(place == 0)
+        def _():
+            pl.semaphore_wait(ready, len(across_place))
+            in_hop().start()
 
     own_copy().wait()
     pltpu.make_async_copy(w, w, weight_sem).wait()
@@ -248,7 +273,12 @@
                 q_copy(block).start()
             if relay and g == 0:
                 detour = jnp.logical_and(jnp.logical_and(place == 1, r == 0), to // 2 != chip)
-                pl.when(detour)(lambda: out_hop(block, to, lax.rem(core + to, 2)).start())
+
+                @pl.when(detour)
+                def _():
+                    out_hop(block, to, lax.rem(core + to, 2)).start()
+                    out_rest(block, to).start()
+
                 pl.when(jnp.logical_not(detour))(lambda: m_copy(block, g).start())
             else:
                 m_copy(block, g).start()
@@ -277,7 +307,7 @@
     def ready_far(g, low, high):
         @pl.loop(0, far_steps)
         def _(step):
-            block = away(lax.rem(step + 2, far_steps))
+            block = away(lax.rem(step + 2, far_steps) if g == 0 else step)
             pl.when(jnp.logical_and(block >= low, block < high))(lambda: finalize(block, g))
 
     @pl.loop(0, chunks)
@@ -490,7 +520,7 @@
             pltpu.VMEM((heads, DH, DH), BF16),
             pltpu.VMEM((heads, 128), F32),
             pltpu.VMEM((rows, width), BF16),
-            pltpu.VMEM((2, rows, width // groups), BF16),
+            pltpu.VMEM((2, rows - 16, width // groups), BF16),
             dma,
             dma((3,)),
             dma,
@@ -508,6 +538,7 @@
             dma((parts,)),
             dma,
             dma((2,)),
+            pltpu.SemaphoreType.REGULAR,
         ],
         compiler_params=pltpu.CompilerParams(
             collective_id=0, has_side_effects=True, vmem_limit_bytes=56 * 1024 * 1024

time: 74.4 us -> 73 us (0.981); the launches traced: 73 us -> 72.9 us
  no operation moved by 1% of the time
where the time goes in v5:
time: 73 us; the launch traced here: 72.9 us
  Pallas kernels  71.5 us (98%)
  local copies, waits for them, and re-layouts  1.32 us (2%)
    pallas_call x1, Pallas kernels, body(): pl.pallas_call(functools.partial(kernel, n_mp, n_seq, heads, rows, groups...  71.5 us

profile of v5, /device:TPU:19, one launch (start us, length us, event | category | flops | bytes accessed | tf_op | source)
XLA Modules:
  0.0 72.9 jit_solution(18401338451632880875)
XLA Ops:
  0.0 71.5 %shard_map.82 = bf16[512,2048]{1,0:T(8,128)(2,1)S(1)} custom-call(bf16[2048,512]{1,0:T(8,128)(2,1)} %tokens.1, bf16[2048,512]{1,0:T(8,128)(2,1)} %wq.1, bf16[2048,512]{1,0:T(8,128)(2,1)} %wk.1, bf16[2048,512]{1,0:T(8,128)(2,1)} %wv.1, bf16[2048,512]{1,0:T(8,128)(2,1)} %wg.1, s32[1,4]{1,0:T(1,128)} %bitcast.5, f32[4,2048]{1,0:T(4,128)} %bitcast.3, ...), custom_call_target="tpu_custom_call" | custom-call | tf_op jit(solution)/shard_map/pallas_call | solution.py:494
  71.5 1.3 %copy.10 = bf16[512,2048]{1,0:T(8,128)(2,1)} copy(bf16[512,2048]{1,0:T(8,128)(2,1)S(1)} %shard_map.82) | data formatting | bytes 4194304

commit v6 on v5

--- a/solution.py
+++ b/solution.py
@@ -42,8 +42,9 @@
     across = [lax.rem(chip + 1, chips) * 2 + core, lax.rem(chip + 1, chips) * 2 + (1 - core)]
 
     barrier = pltpu.get_barrier_semaphore()
-    for other in range(1, n_mp):
-        pl.semaphore_signal(barrier, inc=1, device_id={"mp": lax.rem(me + other, n_mp)}, device_id_type=MESH)
+    greeted = [lax.rem(chip + t, chips) * 2 + core for t in range(1, chips)] + [partner]
+    for there in greeted:
+        pl.semaphore_signal(barrier, inc=1, device_id={"mp": there}, device_id_type=MESH)
 
     across_place = [{"seq": 1 - place}] + [{"mp": there, "seq": 1 - place} for there in across]
 
@@ -67,6 +68,9 @@
         for i, (src, dst) in enumerate(((exponent_in, exponent), (forget_in, forget), (gain_in, gain)))
     ]
 
+    def relative(source, to):
+        return lax.rem(source - to + n_mp, n_mp) - 1
+
     def columns(block):
         return pl.ds(pl.multiple_of(block * width, width), width)
 
@@ -124,15 +128,25 @@
             src_ref=there, dst_ref=there, send_sem=d_send.at[step - 1], recv_sem=d_recv.at[c, step - 1],
             device_id={"mp": partner}, device_id_type=MESH)
 
+    kept_rows = rows - hop_in.shape[0]
+    hop_span = pl.ds(hop_chunk * rows + kept_rows, rows - kept_rows)
+
+    def y_rest():
+        span = pl.ds(hop_chunk * rows, kept_rows)
+        return pltpu.make_async_remote_copy(
+            src_ref=tokens.at[span, :], dst_ref=x.at[span, columns(me)],
+            send_sem=y_send.at[0], recv_sem=y_recv.at[hop_chunk, 0],
+            device_id={"mp": across[0]}, device_id_type=MESH)
+
     def in_hop():
         return pltpu.make_async_remote_copy(
-            src_ref=tokens.at[at_rows(hop_chunk), :], dst_ref=hop_in,
+            src_ref=tokens.at[hop_span, :], dst_ref=hop_in,
             send_sem=y_send.at[0], recv_sem=hop_recv.at[0],
             device_id={"mp": across[0], "seq": 1}, device_id_type=MESH)
 
     def in_next():
         return pltpu.make_async_remote_copy(
-            src_ref=hop_in, dst_ref=x.at[at_rows(hop_chunk), columns(across[0])],
+            src_ref=hop_in, dst_ref=x.at[hop_span, columns(across[0])],
             send_sem=hop_send, recv_sem=y_recv.at[hop_chunk, 0],
             device_id={"seq": 0}, device_id_type=MESH)
 
@@ -147,14 +161,14 @@
     def out_rest(block, to):
         left = rows - hop_rows
         return pltpu.make_async_remote_copy(
-            src_ref=moved.at[pl.ds(pl.multiple_of(block * rows + hop_rows, left), left), pl.ds(0, group_width)],
+            src_ref=moved.at[pl.ds(pl.multiple_of(block * rows + hop_rows, 16), left), pl.ds(0, group_width)],
             dst_ref=got.at[me, pl.ds(hop_rows, left), pl.ds(0, group_width)],
-            send_sem=m_send, recv_sem=m_recv.at[me, 0], device_id={"mp": to}, device_id_type=MESH)
+            send_sem=m_send, recv_sem=m_recv.at[relative(me, to), 0], device_id={"mp": to}, device_id_type=MESH)
 
     def out_next(i):
         return pltpu.make_async_remote_copy(
             src_ref=hop_out.at[i], dst_ref=got.at[across[i], pl.ds(0, hop_rows), pl.ds(0, group_width)],
-            send_sem=hop_send, recv_sem=m_recv.at[across[i], 0],
+            send_sem=hop_send, recv_sem=m_recv.at[relative(across[i], me), 0],
             device_id={"seq": 1}, device_id_type=MESH)
 
     for copy in small:
@@ -167,13 +181,15 @@
         neighbours = place * len(across_place)
     else:
         neighbours = jnp.minimum(place, 1) + jnp.minimum(n_seq - 1 - place, 1)
-    pl.semaphore_wait(barrier, n_mp - 1 + neighbours)
+    pl.semaphore_wait(barrier, len(greeted) + neighbours)
 
     @pl.loop(0, chunks)
     def _(c):
         for step in range(1, chips):
             if relay:
-                pl.when(jnp.logical_or(place > 0, c != hop_chunk))(lambda: y_copy(c, step).start())
+                whole = jnp.logical_or(place > 0, c != hop_chunk)
+                pl.when(whole)(lambda: y_copy(c, step).start())
+                pl.when(jnp.logical_not(whole))(lambda: y_rest().start())
             else:
                 y_copy(c, step).start()
         pl.when(lax.rem(c, 2) == 0)(lambda: p_copy(c // 2).start())
@@ -240,7 +256,7 @@
         to, r = block // parts, lax.rem(block, parts)
         return pltpu.make_async_remote_copy(
             src_ref=moved.at[at_rows(block), group_columns(g)], dst_ref=got.at[me, at_rows(r), group_columns(g)],
-            send_sem=m_send, recv_sem=m_recv.at[me, r],
+            send_sem=m_send, recv_sem=m_recv.at[relative(me, to), r],
             device_id={"mp": to}, device_id_type=MESH)
 
     def q_copy(block):
@@ -434,7 +450,7 @@
     def m_arrival(source, r):
         there = got.at[source, at_rows(r), :]
         return pltpu.make_async_remote_copy(
-            src_ref=there, dst_ref=there, send_sem=m_send, recv_sem=m_recv.at[source, r],
+            src_ref=there, dst_ref=there, send_sem=m_send, recv_sem=m_recv.at[relative(source, me), r],
             device_id={"mp": partner}, device_id_type=MESH)
 
     def q_arrival(r):
@@ -519,8 +535,8 @@
             pltpu.VMEM((heads, DH, DH), BF16),
             pltpu.VMEM((heads, DH, DH), BF16),
             pltpu.VMEM((heads, 128), F32),
-            pltpu.VMEM((rows, width), BF16),
-            pltpu.VMEM((2, rows - 16, width // groups), BF16),
+            pltpu.VMEM((rows - 64, width), BF16),
+            pltpu.VMEM((2, rows - 80, width // groups), BF16),
             dma,
             dma((3,)),
             dma,
@@ -533,7 +549,7 @@
             dma,
             dma((groups,)),
             dma,
-            dma((n_mp, parts)),
+            dma((n_mp - 1, parts)),
             dma,
             dma((parts,)),
             dma,

time: 73 us -> 73 us (level)
  no operation moved by 1% of the time
where the time goes in v6:
time: 73 us; the launch traced here: 72.8 us
  Pallas kernels  71.5 us (98%)
  local copies, waits for them, and re-layouts  1.32 us (2%)
    pallas_call x1, Pallas kernels, body(): pl.pallas_call(functools.partial(kernel, n_mp, n_seq, heads, rows, groups...  71.5 us

profile of v6, /device:TPU:19, one launch (start us, length us, event | category | flops | bytes accessed | tf_op | source)
XLA Modules:
  0.0 72.8 jit_solution(11128547335815424861)
XLA Ops:
  0.0 71.5 %shard_map.82 = bf16[512,2048]{1,0:T(8,128)(2,1)S(1)} custom-call(bf16[2048,512]{1,0:T(8,128)(2,1)} %tokens.1, bf16[2048,512]{1,0:T(8,128)(2,1)} %wq.1, bf16[2048,512]{1,0:T(8,128)(2,1)} %wk.1, bf16[2048,512]{1,0:T(8,128)(2,1)} %wv.1, bf16[2048,512]{1,0:T(8,128)(2,1)} %wg.1, s32[1,4]{1,0:T(1,128)} %bitcast.5, f32[4,2048]{1,0:T(4,128)} %bitcast.3, ...), custom_call_target="tpu_custom_call" | custom-call | tf_op jit(solution)/shard_map/pallas_call | solution.py:510
  71.5 1.3 %copy.10 = bf16[512,2048]{1,0:T(8,128)(2,1)} copy(bf16[512,2048]{1,0:T(8,128)(2,1)S(1)} %shard_map.82) | data formatting | bytes 4194304

commit v7 on v6

--- a/solution.py
+++ b/solution.py
@@ -15,6 +15,12 @@
 
 def contract(a, b, dims):
     return lax.dot_general(a, b, ((dims[0], dims[1]), ((), ())), preferred_element_type=F32)
+
+
+def token_units(n_mp, n_seq, chunks):
+    if n_seq == 2 and n_mp == 4 and chunks > 7:
+        return [(0, 1), (1, 2), (3, 1), (4, 2)] + [(c, 1) for c in range(6, chunks)]
+    return None
 
 
 def kernel(
@@ -89,20 +95,26 @@
     def back_other(step):
         return lax.rem(chip + chips - step, chips) * 2 + (1 - core)
 
+    units = token_units(n_mp, n_seq, chunks)
+    unit_of_hop = hop_chunk if units is None else [first for first, _ in units].index(hop_chunk)
+
+    def unit_rows(i):
+        return at_rows(i) if units is None else pl.ds(units[i][0] * rows, units[i][1] * rows)
+
     def y_copy(c, step):
         return pltpu.make_async_remote_copy(
-            src_ref=tokens.at[at_rows(c), :], dst_ref=x.at[at_rows(c), columns(me)],
+            src_ref=tokens.at[unit_rows(c), :], dst_ref=x.at[unit_rows(c), columns(me)],
             send_sem=y_send.at[step - 1], recv_sem=y_recv.at[c, step - 1],
             device_id={"mp": far(step)}, device_id_type=MESH)
 
     def y_arrival(c, step):
         return pltpu.make_async_remote_copy(
-            src_ref=tokens.at[at_rows(c), :], dst_ref=x.at[at_rows(c), columns(back(step))],
+            src_ref=tokens.at[unit_rows(c), :], dst_ref=x.at[unit_rows(c), columns(back(step))],
             send_sem=y_send.at[step - 1], recv_sem=y_recv.at[c, step - 1],
             device_id={"mp": far(step)}, device_id_type=MESH)
 
     def at_pair(i):
-        return pl.ds(pl.multiple_of(i * 2 * rows, 2 * rows), 2 * rows)
+        return (pl.ds(0, 2 * rows), pl.ds(2 * rows, seq_rows - 2 * rows))[i]
 
     def p_copy(i):
         return pltpu.make_async_remote_copy(
@@ -117,13 +129,13 @@
             device_id={"mp": partner}, device_id_type=MESH)
 
     def d_copy(c, step):
-        there = x.at[at_rows(c), columns(back(step))]
+        there = x.at[unit_rows(c), columns(back(step))]
         return pltpu.make_async_remote_copy(
             src_ref=there, dst_ref=there, send_sem=d_send.at[step - 1], recv_sem=d_recv.at[c, step - 1],
             device_id={"mp": partner}, device_id_type=MESH)
 
     def d_arrival(c, step):
-        there = x.at[at_rows(c), columns(back_other(step))]
+        there = x.at[unit_rows(c), columns(back_other(step))]
         return pltpu.make_async_remote_copy(
             src_ref=there, dst_ref=there, send_sem=d_send.at[step - 1], recv_sem=d_recv.at[c, step - 1],
             device_id={"mp": partner}, device_id_type=MESH)
@@ -135,7 +147,7 @@
         span = pl.ds(hop_chunk * rows, kept_rows)
         return pltpu.make_async_remote_copy(
             src_ref=tokens.at[span, :], dst_ref=x.at[span, columns(me)],
-            send_sem=y_send.at[0], recv_sem=y_recv.at[hop_chunk, 0],
+            send_sem=y_send.at[0], recv_sem=y_recv.at[unit_of_hop, 0],
             device_id={"mp": across[0]}, device_id_type=MESH)
 
     def in_hop():
@@ -147,7 +159,7 @@
     def in_next():
         return pltpu.make_async_remote_copy(
             src_ref=hop_in, dst_ref=x.at[hop_span, columns(across[0])],
-            send_sem=hop_send, recv_sem=y_recv.at[hop_chunk, 0],
+            send_sem=hop_send, recv_sem=y_recv.at[unit_of_hop, 0],
             device_id={"seq": 0}, device_id_type=MESH)
 
     hop_rows = hop_out.shape[1]
@@ -183,16 +195,25 @@
         neighbours = jnp.minimum(place, 1) + jnp.minimum(n_seq - 1 - place, 1)
     pl.semaphore_wait(barrier, len(greeted) + neighbours)
 
-    @pl.loop(0, chunks)
-    def _(c):
+    def send_unit(i, first):
         for step in range(1, chips):
-            if relay:
-                whole = jnp.logical_or(place > 0, c != hop_chunk)
-                pl.when(whole)(lambda: y_copy(c, step).start())
-                pl.when(jnp.logical_not(whole))(lambda: y_rest().start())
+            if relay and first == hop_chunk:
+                pl.when(place > 0)(lambda: y_copy(i, step).start())
+                pl.when(place == 0)(lambda: y_rest().start())
             else:
-                y_copy(c, step).start()
-        pl.when(lax.rem(c, 2) == 0)(lambda: p_copy(c // 2).start())
+                y_copy(i, step).start()
+
+    if units is None:
+        for i in range(chunks):
+            send_unit(i, i)
+    else:
+        for i, (first, _) in enumerate(units):
+            send_unit(i, first)
+            if i < 2:
+                p_copy(i).start()
+    if units is None:
+        for i in range(2):
+            p_copy(i).start()
 
     if relay:
         @pl.when(place == 1)
@@ -226,7 +247,8 @@
         by_rows[c] = turned[:, c * heads : (c + 1) * heads]
 
     def near(c):
-        pl.when(lax.rem(c, 2) == 0)(lambda: p_arrival(c // 2).wait_recv())
+        pl.when(c == 0)(lambda: p_arrival(0).wait_recv())
+        pl.when(c == 2)(lambda: p_arrival(1).wait_recv())
         own_side = pl.ds(pl.multiple_of(chip * 2 * width, 2 * width), 2 * width)
         piece = x[at_rows(c), own_side]
         slot = lax.rem(c, ahead)
@@ -347,9 +369,23 @@
                     enter_state(g)
                     ready_far(g, 0, chunks - 1)
 
-        for step in range(1, chips):
-            y_arrival(c, step).wait_recv()
-            d_copy(c, step).start()
+        def forward(i):
+            for step in range(1, chips):
+                y_arrival(i, step).wait_recv()
+                d_copy(i, step).start()
+
+        def forwarded(i):
+            for step in range(1, chips):
+                d_arrival(i, step).wait_recv()
+
+        def each_unit(act):
+            if units is None:
+                act(c)
+            else:
+                for i, (first, _) in enumerate(units):
+                    pl.when(c == first)(functools.partial(act, i))
+
+        each_unit(forward)
         for step in range(1, chips):
             piece = x[here, columns(back(step))]
             for i in range(4):
@@ -360,8 +396,7 @@
             for g in range(groups):
                 finalize(c - 1, g)
 
-        for step in range(1, chips):
-            d_arrival(c, step).wait_recv()
+        each_unit(forwarded)
 
         if relay:
             @pl.when(jnp.logical_and(place == 1, c == chunks - 2))
@@ -505,6 +540,7 @@
     chunks, parts = seq_rows // rows, own_rows // rows
     groups = 2 if heads % 2 == 0 else 1
     hbm = pl.BlockSpec(memory_space=pltpu.HBM)
+    transfers = len(token_units(n_mp, n_seq, chunks) or range(chunks))
     dma = pltpu.SemaphoreType.DMA
     chips = n_mp // 2
     return pl.pallas_call(
@@ -541,11 +577,11 @@
             dma((3,)),
             dma,
             dma((chips - 1,)),
-            dma((chunks, chips - 1)),
+            dma((transfers, chips - 1)),
             dma,
-            dma((chunks // 2,)),
+            dma((2,)),
             dma((chips - 1,)),
-            dma((chunks, chips - 1)),
+            dma((transfers, chips - 1)),
             dma,
             dma((groups,)),
             dma,

time: 73 us -> 73 us (level)
  no operation moved by 1% of the time
where the time goes in v7:
time: 73 us; the launch traced here: 72.9 us
  Pallas kernels  71.5 us (98%)
  local copies, waits for them, and re-layouts  1.32 us (2%)
    pallas_call x1, Pallas kernels, body(): pl.pallas_call(functools.partial(kernel, n_mp, n_seq, heads, rows, groups...  71.5 us

profile of v7, /device:TPU:19, one launch (start us, length us, event | category | flops | bytes accessed | tf_op | source)
XLA Modules:
  0.0 72.9 jit_solution(10729402941628019688)
XLA Ops:
  0.0 71.5 %shard_map.82 = bf16[512,2048]{1,0:T(8,128)(2,1)S(1)} custom-call(bf16[2048,512]{1,0:T(8,128)(2,1)} %tokens.1, bf16[2048,512]{1,0:T(8,128)(2,1)} %wq.1, bf16[2048,512]{1,0:T(8,128)(2,1)} %wk.1, bf16[2048,512]{1,0:T(8,128)(2,1)} %wv.1, bf16[2048,512]{1,0:T(8,128)(2,1)} %wg.1, s32[1,4]{1,0:T(1,128)} %bitcast.5, f32[4,2048]{1,0:T(4,128)} %bitcast.3, ...), custom_call_target="tpu_custom_call" | custom-call | tf_op jit(solution)/shard_map/pallas_call | solution.py:546
  71.5 1.3 %copy.10 = bf16[512,2048]{1,0:T(8,128)(2,1)} copy(bf16[512,2048]{1,0:T(8,128)(2,1)S(1)} %shard_map.82) | data formatting | bytes 4194304

commit v8 on v6

--- a/solution.py
+++ b/solution.py
@@ -161,7 +161,7 @@
     def out_rest(block, to):
         left = rows - hop_rows
         return pltpu.make_async_remote_copy(
-            src_ref=moved.at[pl.ds(pl.multiple_of(block * rows + hop_rows, 16), left), pl.ds(0, group_width)],
+            src_ref=moved.at[pl.ds(pl.multiple_of(block * rows + hop_rows, left), left), pl.ds(0, group_width)],
             dst_ref=got.at[me, pl.ds(hop_rows, left), pl.ds(0, group_width)],
             send_sem=m_send, recv_sem=m_recv.at[relative(me, to), 0], device_id={"mp": to}, device_id_type=MESH)
 
@@ -536,7 +536,7 @@
             pltpu.VMEM((heads, DH, DH), BF16),
             pltpu.VMEM((heads, 128), F32),
             pltpu.VMEM((rows - 64, width), BF16),
-            pltpu.VMEM((2, rows - 80, width // groups), BF16),
+            pltpu.VMEM((2, rows - 64, width // groups), BF16),
             dma,
             dma((3,)),
             dma,

time: 73 us -> 73.3 us (level)
  no operation moved by 1% of the time
where the time goes in v8:
time: 73.3 us; the launch traced here: 72.5 us
  Pallas kernels  71.1 us (97%)
  local copies, waits for them, and re-layouts  1.32 us (2%)
    pallas_call x1, Pallas kernels, body(): pl.pallas_call(functools.partial(kernel, n_mp, n_seq, heads, rows, groups...  71.1 us

profile of v8, /device:TPU:19, one launch (start us, length us, event | category | flops | bytes accessed | tf_op | source)
XLA Modules:
  0.0 72.5 jit_solution(14390440312044659693)
XLA Ops:
  0.0 71.1 %shard_map.82 = bf16[512,2048]{1,0:T(8,128)(2,1)S(1)} custom-call(bf16[2048,512]{1,0:T(8,128)(2,1)} %tokens.1, bf16[2048,512]{1,0:T(8,128)(2,1)} %wq.1, bf16[2048,512]{1,0:T(8,128)(2,1)} %wk.1, bf16[2048,512]{1,0:T(8,128)(2,1)} %wv.1, bf16[2048,512]{1,0:T(8,128)(2,1)} %wg.1, s32[1,4]{1,0:T(1,128)} %bitcast.5, f32[4,2048]{1,0:T(4,128)} %bitcast.3, ...), custom_call_target="tpu_custom_call" | custom-call | tf_op jit(solution)/shard_map/pallas_call | solution.py:510
  71.1 1.3 %copy.10 = bf16[512,2048]{1,0:T(8,128)(2,1)} copy(bf16[512,2048]{1,0:T(8,128)(2,1)S(1)} %shard_map.82) | data formatting | bytes 4194304
